TPU v7x, 32 devices: a whole 2x2x4 slice. The times are simulated.
32 devices in a mesh: section: 4 (over z), seq: 8 (over y, x, core).
Axes of the slice: x: 2, y: 2, z: 4, core: 2. Of those that a mesh axis runs over, the one named last changes fastest.
Arguments:
- saved: bfloat16 [4, 3, 1024, 2304], P('section', None, 'seq'), may hold values from -8 to 8
- cotangent: bfloat16 [3, 1024, 2304], P(None, 'seq'), may hold values from -0.109375 to 0.109375
- slot_table: int32 [4, 3], P('section'), may hold values from 0 to 2, each once within a row
- gain: float32 [4, 2304], P('section'), may hold values from 0.25 to 1.75
- value_weight: bfloat16 [4, 2304, 1024], P('section'), may hold values from -0.125 to 0.125
- out_weight: bfloat16 [4, 2304, 1024], P('section'), may hold values from -0.1875 to 0.1875
Outputs:
- value_grad: float32 [4, 2304, 1024], P('section', 'seq')
- out_grad: float32 [4, 2304, 1024], P('section', 'seq')
- gain_grad: float32 [4, 2304], P('section')
Inputs may be any that keep to these rules, and one draw needn't show every extreme that they name: `slot_table`: each row names every stash slot once.
All inputs are finite; a program needn't handle non-finite values.
Results may differ from a plain program's by a relative error of at most 0.007.
Values may be sent and summed in bfloat16 or wider, within the bound.
A program may use at most 128 MiB of HBM per device.

v0:
```python
import functools

import jax
import jax.numpy as jnp
from jax import lax
from jax.experimental import pallas as pl
from jax.experimental.pallas import tpu as pltpu
from jax.sharding import PartitionSpec as P

EPSILON = 1e-06


def passed_along(value, axis, steps):
    count = lax.axis_size(axis)
    first, last = (max(0, -steps), min(count, count - steps))
    return lax.ppermute(value, axis, [(source, source + steps) for source in range(first, last)])


def normalize(inputs, gain_row):
    value_rows = inputs.astype(jnp.float32)
    inv_rms = lax.rsqrt(jnp.mean(value_rows * value_rows, axis=-1, keepdims=True) + EPSILON)
    unit_rows = value_rows * inv_rms
    return (unit_rows, inv_rms, (unit_rows * gain_row).astype(jnp.bfloat16))


def input_grads(inputs, grad_out, gain_row, w_value, w_out):
    unit_rows, inv_rms, normed = normalize(inputs, gain_row)
    grad_value = jnp.dot(grad_out, w_out, preferred_element_type=jnp.float32).astype(jnp.bfloat16)
    grad_normed = lax.dot_general(
        grad_value, w_value, (((1,), (1,)), ((), ())), preferred_element_type=jnp.float32
    )
    gain_term = jnp.sum(grad_normed * unit_rows, axis=0)
    grad_unit = grad_normed * gain_row
    grad_in = grad_out.astype(jnp.float32) + inv_rms * (
        grad_unit - unit_rows * jnp.mean(grad_unit * unit_rows, axis=-1, keepdims=True)
    )
    return (grad_in.astype(jnp.bfloat16), grad_value, normed, gain_term)


def arrivals(
    step_index, sent, section_count, section_index, micro_count, cotangent, local_saved, slot_order
):
    if step_index > 0:
        incoming = passed_along(sent, "section", -1)
    else:
        incoming = sent
    micro_index = step_index - (section_count - 1 - section_index)
    active_now = jnp.logical_and(micro_index >= 0, micro_index < micro_count)
    clipped = jnp.clip(micro_index, 0, micro_count - 1)
    top_grad = lax.dynamic_index_in_dim(cotangent, clipped, 0, keepdims=False)
    grad_out = jnp.where(section_index == section_count - 1, top_grad, incoming)
    slot_index = lax.dynamic_index_in_dim(slot_order, clipped, 0, keepdims=False)
    inputs = lax.dynamic_index_in_dim(local_saved, slot_index, 0, keepdims=False)
    return (active_now, clipped, grad_out, inputs)


def per_device(saved, cotangent, slot_table, gain, value_weight, out_weight):
    section_count = lax.axis_size("section")
    section_index = lax.axis_index("section")
    micro_count = slot_table.shape[1]
    local_saved = saved[0]
    slot_order = slot_table[0]
    gain_row = gain[0]
    w_value = value_weight[0]
    w_out = out_weight[0]
    token_rows = cotangent.shape[1]
    model_width = w_value.shape[0]
    inner_width = w_value.shape[1]
    sent = jnp.zeros((token_rows, model_width), jnp.bfloat16)
    gain_acc = jnp.zeros((model_width,), jnp.float32)
    out_stash = jnp.zeros((micro_count, token_rows, model_width), jnp.bfloat16)
    value_stash = jnp.zeros((micro_count, token_rows, inner_width), jnp.bfloat16)
    for step_index in range(micro_count + section_count - 1):
        active_now, clipped, grad_out, inputs = arrivals(
            step_index,
            sent,
            section_count,
            section_index,
            micro_count,
            cotangent,
            local_saved,
            slot_order,
        )

        def working(carried):
            grad_in, grad_value, normed, gain_term = input_grads(
                inputs, grad_out, gain_row, w_value, w_out
            )
            new_out = lax.dynamic_update_index_in_dim(carried[2], grad_out, clipped, 0)
            new_value = lax.dynamic_update_index_in_dim(carried[3], grad_value, clipped, 0)
            return (grad_in, carried[1] + gain_term, new_out, new_value)

        def resting(carried):
            return carried

        sent, gain_acc, out_stash, value_stash = lax.cond(
            active_now, working, resting, (sent, gain_acc, out_stash, value_stash)
        )
    ordered = jnp.take(local_saved, slot_order, axis=0).reshape(
        micro_count * token_rows, model_width
    )
    unit_all, inv_all, normed_all = normalize(ordered, gain_row)
    values_all = jnp.dot(normed_all, w_value, preferred_element_type=jnp.float32).astype(
        jnp.bfloat16
    )
    grads_all = out_stash.reshape(micro_count * token_rows, model_width)
    grad_values = value_stash.reshape(micro_count * token_rows, inner_width)
    value_acc = lax.dot_general(
        normed_all, grad_values, (((0,), (0,)), ((), ())), preferred_element_type=jnp.float32
    )
    out_acc = lax.dot_general(
        grads_all, values_all, (((0,), (0,)), ((), ())), preferred_element_type=jnp.float32
    )
    value_grad, out_grad = (
        lax.psum_scatter(value_acc, "seq", scatter_dimension=0, tiled=True),
        lax.psum_scatter(out_acc, "seq", scatter_dimension=0, tiled=True),
    )
    gain_total = lax.psum(gain_acc, "seq")
    return (value_grad[None], out_grad[None], gain_total[None])


TILE = 256
LANES = 128
VMEM_BYTES = 60 * 1024 * 1024


def flipped(index, bits, count):
    total, unit = 0, 1
    while unit < count:
        total = total + ((index // unit + (bits // unit) % 2) % 2) * unit
        unit *= 2
    return total


def tile_at(index, size=TILE):
    return pl.ds(pl.multiple_of(index * size, size), size)


def fused_kernel(
    peers,
    sections,
    slot_ref,
    saved_ref,
    cot_ref,
    gain_ref,
    wv_ref,
    wo_ref,
    vg_ref,
    og_ref,
    gg_ref,
    inv_buf,
    grad_buf,
    pass_buf,
    gn_buf,
    rows_all,
    turned,
    cols_all,
    gain_all,
    rows_send,
    rows_recv,
    cols_send,
    cols_recv,
    down_send,
    down_recv,
    gain_send,
    gain_recv,
):
    section = lax.axis_index("section")
    me = lax.axis_index("seq")
    micro, tokens, width = cot_ref.shape
    inner = wv_ref.shape[1]
    share = width // peers
    wide, narrow = width // TILE, inner // TILE
    top = section == sections - 1

    def peer(bits):
        return {"seq": flipped(me, bits, peers)}

    def row_copy(kind, m, owner, sem, target):
        place = rows_all.at[kind, m, tile_at(owner, tokens)]
        return pltpu.make_async_remote_copy(
            src_ref=place,
            dst_ref=place,
            send_sem=rows_send.at[kind, m, sem],
            recv_sem=rows_recv.at[kind, m, sem],
            device_id=target,
            device_id_type=pl.DeviceIdType.MESH,
        )

    def own_rows(kind, m, bits):
        return row_copy(kind, m, me, bits, peer(bits))

    def relayed_rows(kind, m, bits):
        return row_copy(kind, m, flipped(me, bits, peers), bits + 1, peer(1))

    def arriving_rows(kind, m, bits):
        return row_copy(kind, m, flipped(me, bits, peers), bits, peer(bits))

    def col_copy(kind, m, owner, bits):
        return pltpu.make_async_remote_copy(
            src_ref=turned.at[kind, m, tile_at(flipped(me, bits, peers), share)],
            dst_ref=cols_all.at[kind, m, :, tile_at(owner, tokens)],
            send_sem=cols_send.at[kind, m, bits],
            recv_sem=cols_recv.at[kind, m, bits],
            device_id=peer(bits),
            device_id_type=pl.DeviceIdType.MESH,
        )

    def down_copy(m, target):
        return pltpu.make_async_remote_copy(
            src_ref=pass_buf.at[m],
            dst_ref=grad_buf.at[m],
            send_sem=down_send.at[m],
            recv_sem=down_recv.at[m],
            device_id={"section": target},
            device_id_type=pl.DeviceIdType.MESH,
        )

    def gain_copy(owner, bits):
        return pltpu.make_async_remote_copy(
            src_ref=gain_all.at[owner],
            dst_ref=gain_all.at[owner],
            send_sem=gain_send.at[bits],
            recv_sem=gain_recv.at[bits],
            device_id=peer(bits),
            device_id_type=pl.DeviceIdType.MESH,
        )

    barrier = pltpu.get_barrier_semaphore()
    for bits in range(1, peers):
        pl.semaphore_signal(
            barrier, inc=1, device_id=peer(bits), device_id_type=pl.DeviceIdType.MESH
        )

    @pl.when(section > 0)
    def _():
        pl.semaphore_signal(
            barrier,
            inc=1,
            device_id={"section": section - 1},
            device_id_type=pl.DeviceIdType.MESH,
        )

    @pl.when(section < sections - 1)
    def _():
        pl.semaphore_signal(
            barrier,
            inc=1,
            device_id={"section": section + 1},
            device_id_type=pl.DeviceIdType.MESH,
        )

    pl.semaphore_wait(
        barrier,
        peers - 1
        + (section > 0).astype(jnp.int32)
        + (section < sections - 1).astype(jnp.int32),
    )

    gain_all[me] = jnp.zeros((1, width), jnp.float32)
    vg_ref[...] = jnp.zeros_like(vg_ref)
    og_ref[...] = jnp.zeros_like(og_ref)

    def scales(m, carry):
        slot = slot_ref[0, m]

        def squares(j, total):
            x = saved_ref[slot, :, tile_at(j)].astype(jnp.float32)
            return total + jnp.sum(x * x, axis=1, keepdims=True)

        total = lax.fori_loop(0, wide, squares, jnp.zeros((tokens, 1), jnp.float32))
        inv_buf[m] = lax.rsqrt(total / width + EPSILON)
        return carry

    lax.fori_loop(0, micro, scales, 0)

    def send_cols(kind, m):
        cols_all[kind, m, :, tile_at(me, tokens)] = turned[kind, m, tile_at(me, share)]
        for bits in range(1, peers):
            col_copy(kind, m, me, bits).start()

    def send_rows(kind, m):
        for bits in (*range(2, peers, 2), 1):
            own_rows(kind, m, bits).start()

    def values(m):
        slot = slot_ref[0, m]
        inv = inv_buf[m]

        def norm(j, carry):
            x = saved_ref[slot, :, tile_at(j)].astype(jnp.float32)
            n = (x * inv * gain_ref[:, tile_at(j)]).astype(jnp.bfloat16)
            pass_tile[:, tile_at(j)] = n
            turned[0, m, tile_at(j)] = n.T
            return carry

        lax.fori_loop(0, wide, norm, 0)
        send_cols(0, m)

        def project(j, carry):
            rows_all[0, m, tile_at(me, tokens), tile_at(j)] = jnp.dot(
                pass_tile[...], wv_ref[:, tile_at(j)], preferred_element_type=jnp.float32
            ).astype(jnp.bfloat16)
            return carry

        lax.fori_loop(0, narrow, project, 0)
        send_rows(0, m)

    pass_tile = gn_buf[0]
    gn = gn_buf[1]

    def chain(m):
        slot = slot_ref[0, m]
        inv = inv_buf[m]

        @pl.when(top)
        def _():
            grad_buf[m] = cot_ref[m]

        @pl.when(section < sections - 1)
        def _():
            down_copy(m, section + 1).wait_recv()

        def project(j, carry):
            rows_all[1, m, tile_at(me, tokens), tile_at(j)] = jnp.dot(
                grad_buf[m], wo_ref[:, tile_at(j)], preferred_element_type=jnp.float32
            ).astype(jnp.bfloat16)
            return carry

        lax.fori_loop(0, narrow, project, 0)
        send_rows(1, m)

        def back(j, total):
            term = lax.dot_general(
                rows_all[1, m, tile_at(me, tokens)],
                wv_ref[tile_at(j)],
                (((1,), (1,)), ((), ())),
                preferred_element_type=jnp.float32,
            )
            unit = saved_ref[slot, :, tile_at(j)].astype(jnp.float32) * inv
            gn[:, tile_at(j)] = term
            both = term * unit
            gain_all[me, :, tile_at(j)] += jnp.sum(both, axis=0, keepdims=True)
            return total + jnp.sum(both * gain_ref[:, tile_at(j)], axis=1, keepdims=True)

        total = lax.fori_loop(0, wide, back, jnp.zeros((tokens, 1), jnp.float32))
        mean = total / width

        @pl.when(section > 0)
        def _():
            def step(j, carry):
                unit = saved_ref[slot, :, tile_at(j)].astype(jnp.float32) * inv
                grad_unit = gn[:, tile_at(j)] * gain_ref[:, tile_at(j)]
                pass_buf[m, :, tile_at(j)] = (
                    grad_buf[m, :, tile_at(j)].astype(jnp.float32)
                    + inv * (grad_unit - unit * mean)
                ).astype(jnp.bfloat16)
                return carry

            lax.fori_loop(0, wide, step, 0)
            down_copy(m, section - 1).start()

        def turn(j, carry):
            turned[1, m, tile_at(j)] = grad_buf[m, :, tile_at(j)].T
            return carry

        lax.fori_loop(0, wide, turn, 0)
        send_cols(1, m)

    def stage(t, carry):
        at_top = top.astype(jnp.int32)
        chained = at_top * (1 - t % 2) + (1 - at_top) * (t // micro)
        m = at_top * (t // 2) + (1 - at_top) * (t % micro)

        @pl.when(chained == 1)
        def _():
            chain(m)

        @pl.when(chained == 0)
        def _():
            values(m)

        return carry

    lax.fori_loop(0, 2 * micro, stage, 0)
    for bits in range(1, peers):
        gain_copy(me, bits).start()

    def finish(m, carry):
        for kind in (0, 1):
            for bits in range(2, peers, 2):
                arriving_rows(kind, m, bits).wait_recv()
                relayed_rows(kind, m, bits).start()
        for kind in (0, 1):
            for bits in range(1, peers):
                col_copy(kind, m, flipped(me, bits, peers), bits).wait_recv()
        for kind in (0, 1):
            for bits in range(1, peers, 2):
                arriving_rows(kind, m, bits).wait_recv()

        def weight(j, inside):
            vg_ref[:, tile_at(j)] += jnp.dot(
                cols_all[0, m], rows_all[1, m, :, tile_at(j)], preferred_element_type=jnp.float32
            )
            og_ref[:, tile_at(j)] += jnp.dot(
                cols_all[1, m], rows_all[0, m, :, tile_at(j)], preferred_element_type=jnp.float32
            )
            return inside

        lax.fori_loop(0, narrow, weight, 0)
        return carry

    lax.fori_loop(0, micro, finish, 0)
    for bits in range(1, peers):
        gain_copy(flipped(me, bits, peers), bits).wait_recv()
    gained = gain_all[0]
    for owner in range(1, peers):
        gained = gained + gain_all[owner]
    gg_ref[...] = gained

    def drain(m, carry):
        for kind in (0, 1):
            for bits in range(1, peers):
                col_copy(kind, m, me, bits).wait_send()
            for bits in (1, *range(2, peers, 2)):
                own_rows(kind, m, bits).wait_send()
            for bits in range(2, peers, 2):
                relayed_rows(kind, m, bits).wait_send()

        @pl.when(section > 0)
        def _():
            down_copy(m, section - 1).wait_send()

        return carry

    lax.fori_loop(0, micro, drain, 0)
    for bits in range(1, peers):
        gain_copy(me, bits).wait_send()


def fused(mesh, saved, cotangent, slot_table, gain, value_weight, out_weight):
    peers, sections = mesh.shape["seq"], mesh.shape["section"]
    micro, tokens, width = cotangent.shape
    inner = value_weight.shape[2]
    share = width // peers
    hbm = pl.BlockSpec(memory_space=pltpu.VMEM)
    value_grad, out_grad, gain_grad = pl.pallas_call(
        functools.partial(fused_kernel, peers, sections),
        out_shape=(
            jax.ShapeDtypeStruct((share, inner), jnp.float32),
            jax.ShapeDtypeStruct((share, inner), jnp.float32),
            jax.ShapeDtypeStruct((1, width), jnp.float32),
        ),
        in_specs=[pl.BlockSpec(memory_space=pltpu.SMEM)] + [hbm] * 5,
        out_specs=(hbm, hbm, hbm),
        scratch_shapes=[
            pltpu.VMEM((micro, tokens, 1), jnp.float32),
            pltpu.VMEM((micro, tokens, width), jnp.bfloat16),
            pltpu.VMEM((micro, tokens, width), jnp.bfloat16),
            (pltpu.VMEM((tokens, width), jnp.bfloat16), pltpu.VMEM((tokens, width), jnp.float32)),
            pltpu.VMEM((2, micro, peers * tokens, inner), jnp.bfloat16),
            pltpu.VMEM((2, micro, width, tokens), jnp.bfloat16),
            pltpu.VMEM((2, micro, share, peers * tokens), jnp.bfloat16),
            pltpu.VMEM((peers, 1, width), jnp.float32),
            pltpu.SemaphoreType.DMA((2, micro, peers)),
            pltpu.SemaphoreType.DMA((2, micro, peers)),
            pltpu.SemaphoreType.DMA((2, micro, peers)),
            pltpu.SemaphoreType.DMA((2, micro, peers)),
            pltpu.SemaphoreType.DMA((micro,)),
            pltpu.SemaphoreType.DMA((micro,)),
            pltpu.SemaphoreType.DMA((peers,)),
            pltpu.SemaphoreType.DMA((peers,)),
        ],
        compiler_params=pltpu.CompilerParams(
            collective_id=0, has_side_effects=True, vmem_limit_bytes=VMEM_BYTES
        ),
    )(slot_table, saved[0], cotangent, gain, value_weight[0], out_weight[0])
    return value_grad[None], out_grad[None], gain_grad


def fits(mesh, saved, cotangent, slot_table, gain, value_weight, out_weight):
    peers = mesh.shape["seq"]
    micro, tokens, width = cotangent.shape
    inner = value_weight.shape[2]
    held = 4 * width * inner + 4 * micro * tokens * (2 * width + inner * peers)
    held += 4 * micro * tokens * width * 3 + 8 * (width // peers) * inner + 6 * tokens * width
    return (
        peers & (peers - 1) == 0
        and tokens % LANES == 0
        and width % TILE == 0
        and inner % TILE == 0
        and width % (16 * peers) == 0
        and held < VMEM_BYTES - 4 * 1024 * 1024
    )


def on_device(mesh, *arrays):
    if fits(mesh, *arrays):
        return fused(mesh, *arrays)
    return per_device(*arrays)


def solution(mesh):
    in_specs = (
        P("section", None, "seq", None),
        P(None, "seq", None),
        P("section", None),
        P("section", None),
        P("section", None, None),
        P("section", None, None),
    )
    out_specs = (P("section", "seq", None), P("section", "seq", None), P("section", None))
    return jax.shard_map(
        functools.partial(on_device, mesh), mesh=mesh, in_specs=in_specs, out_specs=out_specs, check_vma=False
    )
```

profile of v0, /device:TPU:0, one launch (start us, length us, event | category | flops | bytes accessed | tf_op | source)
XLA Modules:
  0.0 135.8 jit_solution(6562707774510494726)
XLA Ops:
  0.6 131.0 %shard_map.85 = (f32[288,1024]{1,0:T(8,128)}, f32[288,1024]{1,0:T(8,128)}, f32[1,2304]{1,0:T(1,128)}) custom-call(s32[1,3]{1,0:T(1,128)} %slot_ref.1, bf16[3,128,2304]{2,1,0:T(8,128)(2,1)} %bitcast.7, bf16[3,128,2304]{2,1,0:T(8,128)(2,1)} %cot_ref.1, f32[1,2304]{1,0:T(1,128)} %gain_ref.1, bf16[2304,1024]{1,0:T(8,128)(2,1)} %bitcast.5, bf16[2304,1024]{1,0:T(8,128)(2,1)} %bitcast.6), custom_call_target="tpu_custom_call" | custom-call | tf_op jit(solution)/shard_map/pallas_call | solution.py:447
  131.6 0.0 copy-start
  131.6 2.5 %copy.12 = f32[1,288,1024]{2,1,0:T(8,128)} copy(f32[1,288,1024]{2,1,0:T(8,128)} %bitcast.9) | data formatting | bytes 2359296
  134.2 0.0 copy-done
  134.2 0.0 copy-start.1
  134.2 1.0 copy.13
  135.2 0.0 copy-done.1
  135.2 0.6 copy.14
Async XLA Ops:
  131.6 2.5 %copy-start = (f32[288,1024]{1,0:T(8,128)S(1)}, f32[288,1024]{1,0:T(8,128)}, u32[]{:S(2)}) copy-start(f32[288,1024]{1,0:T(8,128)} %get-tuple-element.7) | copy-start | bytes 3538948
  134.2 1.0 copy-start.1
where the time goes:
time: 136 us
  Pallas kernels  131 us (96%)
  local copies, waits for them, and re-layouts  4.12 us (3%)
    pallas_call x1, Pallas kernels, fused(): pl.pallas_call(functools.partial(fused_kernel, peers, sections), out_shap...  131 us
    unnamed x7, local copies, waits for them, and re-layouts  4.12 us

commit v1 on v0

--- a/solution.py
+++ b/solution.py
@@ -121,6 +121,7 @@
 
 TILE = 256
 LANES = 128
+CHUNKS = 2
 VMEM_BYTES = 60 * 1024 * 1024
 
 
@@ -140,79 +141,131 @@
     peers,
     sections,
     slot_ref,
-    saved_ref,
-    cot_ref,
+    saved_hbm,
+    cot_hbm,
     gain_ref,
-    wv_ref,
-    wo_ref,
+    wv_hbm,
+    wo_hbm,
     vg_ref,
     og_ref,
     gg_ref,
+    saved_ref,
+    wv_ref,
+    wo_ref,
     inv_buf,
     grad_buf,
     pass_buf,
-    gn_buf,
+    normed,
+    gn,
     rows_all,
     turned,
     cols_all,
+    acc,
+    part_out,
+    part_in,
     gain_all,
+    load_sem,
     rows_send,
     rows_recv,
     cols_send,
     cols_recv,
     down_send,
     down_recv,
+    part_send,
+    part_recv,
     gain_send,
     gain_recv,
 ):
     section = lax.axis_index("section")
     me = lax.axis_index("seq")
-    micro, tokens, width = cot_ref.shape
+    micro, tokens, width = grad_buf.shape
     inner = wv_ref.shape[1]
     share = width // peers
     wide, narrow = width // TILE, inner // TILE
+    chunk = tokens // CHUNKS
+    steps = micro * CHUNKS
     top = section == sections - 1
+    near = (peers // 4, peers // 2)
+    far = (peers // 2, peers // 4)
 
     def peer(bits):
         return {"seq": flipped(me, bits, peers)}
 
-    def row_copy(kind, m, owner, sem, target):
-        place = rows_all.at[kind, m, tile_at(owner, tokens)]
+    def coordinate(device, bit):
+        return (device // bit) % 2
+
+    def place(kind, device):
+        return coordinate(device, near[kind]) * 2 + device % 2
+
+    def rows_at(kind, m, h, owner):
+        if kind == 1:
+            return rows_all.at[kind, m, tile_at(place(kind, owner), tokens)]
+        return rows_all.at[kind, m, tile_at(place(kind, owner) * CHUNKS + h, chunk)]
+
+    def row_copy(kind, m, h, owner, way, bits):
+        spot = rows_at(kind, m, h, owner)
         return pltpu.make_async_remote_copy(
-            src_ref=place,
-            dst_ref=place,
-            send_sem=rows_send.at[kind, m, sem],
-            recv_sem=rows_recv.at[kind, m, sem],
-            device_id=target,
-            device_id_type=pl.DeviceIdType.MESH,
-        )
-
-    def own_rows(kind, m, bits):
-        return row_copy(kind, m, me, bits, peer(bits))
-
-    def relayed_rows(kind, m, bits):
-        return row_copy(kind, m, flipped(me, bits, peers), bits + 1, peer(1))
-
-    def arriving_rows(kind, m, bits):
-        return row_copy(kind, m, flipped(me, bits, peers), bits, peer(bits))
-
-    def col_copy(kind, m, owner, bits):
-        return pltpu.make_async_remote_copy(
-            src_ref=turned.at[kind, m, tile_at(flipped(me, bits, peers), share)],
-            dst_ref=cols_all.at[kind, m, :, tile_at(owner, tokens)],
-            send_sem=cols_send.at[kind, m, bits],
-            recv_sem=cols_recv.at[kind, m, bits],
+            src_ref=spot,
+            dst_ref=spot,
+            send_sem=rows_send.at[kind, m, h, way],
+            recv_sem=rows_recv.at[kind, m, h, way],
             device_id=peer(bits),
             device_id_type=pl.DeviceIdType.MESH,
         )
 
-    def down_copy(m, target):
+    def own_to_core(kind, m, h):
+        return row_copy(kind, m, h, me, 0, 1)
+
+    def own_to_chip(kind, m, h):
+        return row_copy(kind, m, h, me, 1, near[kind])
+
+    def relay(kind, m, h):
+        return row_copy(kind, m, h, flipped(me, near[kind], peers), 2, 1)
+
+    def from_core(kind, m, h):
+        return row_copy(kind, m, h, flipped(me, 1, peers), 0, 1)
+
+    def from_chip(kind, m, h):
+        return row_copy(kind, m, h, flipped(me, near[kind], peers), 1, near[kind])
+
+    def from_relay(kind, m, h):
+        return row_copy(kind, m, h, flipped(me, near[kind] + 1, peers), 2, 1)
+
+    def block_of(kind, device, b):
+        return device + (b - coordinate(device, far[kind])) * far[kind]
+
+    def col_copy(kind, m, owner, bits, b):
+        target = flipped(me, bits, peers)
         return pltpu.make_async_remote_copy(
-            src_ref=pass_buf.at[m],
-            dst_ref=grad_buf.at[m],
-            send_sem=down_send.at[m],
-            recv_sem=down_recv.at[m],
+            src_ref=turned.at[kind, m, tile_at(block_of(kind, target, b), share)],
+            dst_ref=cols_all.at[kind, m, b, :, tile_at(place(kind, owner), tokens)],
+            send_sem=cols_send.at[kind, m, bits, b],
+            recv_sem=cols_recv.at[kind, m, bits, b],
+            device_id=peer(bits),
+            device_id_type=pl.DeviceIdType.MESH,
+        )
+
+    def ways(kind):
+        return (near[kind], near[kind] + 1, 1)
+
+    def down_copy(k, target):
+        spot = tile_at(k % CHUNKS, chunk)
+        return pltpu.make_async_remote_copy(
+            src_ref=pass_buf.at[k // CHUNKS, spot],
+            dst_ref=grad_buf.at[k // CHUNKS, spot],
+            send_sem=down_send.at[k],
+            recv_sem=down_recv.at[k],
             device_id={"section": target},
+            device_id_type=pl.DeviceIdType.MESH,
+        )
+
+    def part_copy(kind, j):
+        return pltpu.make_async_remote_copy(
+            src_ref=part_out.at[kind, j],
+            dst_ref=part_in.at[kind, j],
+            send_sem=part_send.at[kind, j],
+            recv_sem=part_recv.at[kind, j],
+            device_id=peer(far[kind]),
             device_id_type=pl.DeviceIdType.MESH,
         )
 
@@ -226,6 +279,19 @@
             device_id_type=pl.DeviceIdType.MESH,
         )
 
+    load_saved = pltpu.make_async_copy(saved_hbm, saved_ref, load_sem.at[0])
+    load_wo = pltpu.make_async_copy(wo_hbm, wo_ref, load_sem.at[1])
+    load_wv = pltpu.make_async_copy(wv_hbm, wv_ref, load_sem.at[2])
+    load_cot = pltpu.make_async_copy(cot_hbm, grad_buf, load_sem.at[3])
+    load_saved.start()
+
+    @pl.when(top)
+    def _():
+        load_cot.start()
+
+    load_wo.start()
+    load_wv.start()
+
     barrier = pltpu.get_barrier_semaphore()
     for bits in range(1, peers):
         pl.semaphore_signal(
@@ -250,6 +316,28 @@
             device_id_type=pl.DeviceIdType.MESH,
         )
 
+    gain_all[me] = jnp.zeros((1, width), jnp.float32)
+    load_saved.wait()
+
+    def scales(m, carry):
+        slot = slot_ref[0, m]
+
+        def squares(j, total):
+            x = saved_ref[slot, :, tile_at(j)].astype(jnp.float32)
+            return total + jnp.sum(x * x, axis=1, keepdims=True)
+
+        total = lax.fori_loop(0, wide, squares, jnp.zeros((tokens, 1), jnp.float32))
+        inv_buf[m] = lax.rsqrt(total / width + EPSILON)
+        return carry
+
+    lax.fori_loop(0, micro, scales, 0)
+
+    @pl.when(top)
+    def _():
+        load_cot.wait()
+
+    load_wo.wait()
+    load_wv.wait()
     pl.semaphore_wait(
         barrier,
         peers - 1
@@ -257,31 +345,14 @@
         + (section < sections - 1).astype(jnp.int32),
     )
 
-    gain_all[me] = jnp.zeros((1, width), jnp.float32)
-    vg_ref[...] = jnp.zeros_like(vg_ref)
-    og_ref[...] = jnp.zeros_like(og_ref)
-
-    def scales(m, carry):
-        slot = slot_ref[0, m]
-
-        def squares(j, total):
-            x = saved_ref[slot, :, tile_at(j)].astype(jnp.float32)
-            return total + jnp.sum(x * x, axis=1, keepdims=True)
-
-        total = lax.fori_loop(0, wide, squares, jnp.zeros((tokens, 1), jnp.float32))
-        inv_buf[m] = lax.rsqrt(total / width + EPSILON)
-        return carry
-
-    lax.fori_loop(0, micro, scales, 0)
-
     def send_cols(kind, m):
-        cols_all[kind, m, :, tile_at(me, tokens)] = turned[kind, m, tile_at(me, share)]
-        for bits in range(1, peers):
-            col_copy(kind, m, me, bits).start()
-
-    def send_rows(kind, m):
-        for bits in (*range(2, peers, 2), 1):
-            own_rows(kind, m, bits).start()
+        for bits in ways(kind):
+            for b in range(2):
+                col_copy(kind, m, me, bits, b).start()
+        for b in range(2):
+            cols_all[kind, m, b, :, tile_at(place(kind, me), tokens)] = turned[
+                kind, m, tile_at(block_of(kind, me, b), share)
+            ]
 
     def values(m):
         slot = slot_ref[0, m]
@@ -290,7 +361,7 @@
         def norm(j, carry):
             x = saved_ref[slot, :, tile_at(j)].astype(jnp.float32)
             n = (x * inv * gain_ref[:, tile_at(j)]).astype(jnp.bfloat16)
-            pass_tile[:, tile_at(j)] = n
+            normed[:, tile_at(j)] = n
             turned[0, m, tile_at(j)] = n.T
             return carry
 
@@ -298,83 +369,151 @@
         send_cols(0, m)
 
         def project(j, carry):
-            rows_all[0, m, tile_at(me, tokens), tile_at(j)] = jnp.dot(
-                pass_tile[...], wv_ref[:, tile_at(j)], preferred_element_type=jnp.float32
+            rows_all[1, m, tile_at(place(1, me), tokens), tile_at(j)] = jnp.dot(
+                normed[...], wv_ref[:, tile_at(j)], preferred_element_type=jnp.float32
             ).astype(jnp.bfloat16)
             return carry
 
         lax.fori_loop(0, narrow, project, 0)
-        send_rows(0, m)
-
-    pass_tile = gn_buf[0]
-    gn = gn_buf[1]
-
-    def chain(m):
+        own_to_chip(1, m, 0).start()
+        own_to_core(1, m, 0).start()
+
+    def turn(m):
+        def tile(j, carry):
+            turned[1, m, tile_at(j)] = grad_buf[m, :, tile_at(j)].T
+            return carry
+
+        lax.fori_loop(0, wide, tile, 0)
+        send_cols(1, m)
+
+    def chain(k):
+        m, h = k // CHUNKS, k % CHUNKS
+        here = tile_at(h, chunk)
         slot = slot_ref[0, m]
-        inv = inv_buf[m]
-
-        @pl.when(top)
-        def _():
-            grad_buf[m] = cot_ref[m]
+        inv = inv_buf[m, here]
+        mine = tile_at(place(0, me) * CHUNKS + h, chunk)
 
         @pl.when(section < sections - 1)
         def _():
-            down_copy(m, section + 1).wait_recv()
+            down_copy(k, section + 1).wait_recv()
 
         def project(j, carry):
-            rows_all[1, m, tile_at(me, tokens), tile_at(j)] = jnp.dot(
-                grad_buf[m], wo_ref[:, tile_at(j)], preferred_element_type=jnp.float32
+            rows_all[0, m, mine, tile_at(j)] = jnp.dot(
+                grad_buf[m, here], wo_ref[:, tile_at(j)], preferred_element_type=jnp.float32
             ).astype(jnp.bfloat16)
             return carry
 
         lax.fori_loop(0, narrow, project, 0)
-        send_rows(1, m)
+        own_to_chip(0, m, h).start()
+        own_to_core(0, m, h).start()
+
+        @pl.when(jnp.logical_and(section == 0, h == CHUNKS - 1))
+        def _():
+            turn(m)
 
         def back(j, total):
             term = lax.dot_general(
-                rows_all[1, m, tile_at(me, tokens)],
+                rows_all[0, m, mine],
                 wv_ref[tile_at(j)],
                 (((1,), (1,)), ((), ())),
                 preferred_element_type=jnp.float32,
             )
-            unit = saved_ref[slot, :, tile_at(j)].astype(jnp.float32) * inv
+            unit = saved_ref[slot, here, tile_at(j)].astype(jnp.float32) * inv
             gn[:, tile_at(j)] = term
             both = term * unit
             gain_all[me, :, tile_at(j)] += jnp.sum(both, axis=0, keepdims=True)
             return total + jnp.sum(both * gain_ref[:, tile_at(j)], axis=1, keepdims=True)
 
-        total = lax.fori_loop(0, wide, back, jnp.zeros((tokens, 1), jnp.float32))
+        total = lax.fori_loop(0, wide, back, jnp.zeros((chunk, 1), jnp.float32))
         mean = total / width
 
         @pl.when(section > 0)
         def _():
             def step(j, carry):
-                unit = saved_ref[slot, :, tile_at(j)].astype(jnp.float32) * inv
+                unit = saved_ref[slot, here, tile_at(j)].astype(jnp.float32) * inv
                 grad_unit = gn[:, tile_at(j)] * gain_ref[:, tile_at(j)]
-                pass_buf[m, :, tile_at(j)] = (
-                    grad_buf[m, :, tile_at(j)].astype(jnp.float32)
+                pass_buf[m, here, tile_at(j)] = (
+                    grad_buf[m, here, tile_at(j)].astype(jnp.float32)
                     + inv * (grad_unit - unit * mean)
                 ).astype(jnp.bfloat16)
                 return carry
 
             lax.fori_loop(0, wide, step, 0)
-            down_copy(m, section - 1).start()
-
-        def turn(j, carry):
-            turned[1, m, tile_at(j)] = grad_buf[m, :, tile_at(j)].T
-            return carry
-
-        lax.fori_loop(0, wide, turn, 0)
-        send_cols(1, m)
+            down_copy(k, section - 1).start()
+
+        @pl.when(jnp.logical_and(section > 0, h == CHUNKS - 1))
+        def _():
+            turn(m)
+
+    def relay_values():
+        def one(m, carry):
+            from_chip(1, m, 0).wait_recv()
+            relay(1, m, 0).start()
+            return carry
+
+        lax.fori_loop(0, micro, one, 0)
+
+    def relay_grads(k):
+        from_chip(0, k // CHUNKS, k % CHUNKS).wait_recv()
+        relay(0, k // CHUNKS, k % CHUNKS).start()
+
+    def gather(kind, m):
+        for bits in ways(kind):
+            for b in range(2):
+                col_copy(kind, m, flipped(me, bits, peers), bits, b).wait_recv()
+        for h in range(CHUNKS if kind == 0 else 1):
+            from_core(kind, m, h).wait_recv()
+            from_relay(kind, m, h).wait_recv()
+
+    def product(kind, m, b, j):
+        return jnp.dot(
+            cols_all[kind, m, b],
+            rows_all[kind, m, :, tile_at(j)],
+            preferred_element_type=jnp.float32,
+        )
+
+    def weights(m):
+        for kind in (0, 1):
+            gather(kind, m)
+
+            def tile(i, carry):
+                b, j = i // narrow, i % narrow
+                acc[kind, b, :, tile_at(j)] += product(kind, m, b, j)
+                return carry
+
+            lax.fori_loop(0, 2 * narrow, tile, 0)
+
+    @pl.when(section > 0)
+    def _():
+        acc[...] = jnp.zeros_like(acc)
 
     def stage(t, carry):
         at_top = top.astype(jnp.int32)
-        chained = at_top * (1 - t % 2) + (1 - at_top) * (t // micro)
-        m = at_top * (t // 2) + (1 - at_top) * (t % micro)
+        paired = (t < 2 * micro).astype(jnp.int32)
+        chained = at_top * (1 - paired * (t % 2)) + (1 - at_top) * (t >= micro).astype(jnp.int32)
+        k = at_top * (paired * (t // 2) + (1 - paired) * (t - micro)) + (1 - at_top) * (t - micro)
+        m = at_top * (t // 2) + (1 - at_top) * t
 
         @pl.when(chained == 1)
         def _():
-            chain(m)
+            @pl.when(jnp.logical_and(section == 0, k == 0))
+            def _():
+                acc[...] = jnp.zeros_like(acc)
+                relay_values()
+
+            chain(k)
+
+            @pl.when(jnp.logical_and(section == 0, k > 0))
+            def _():
+                relay_grads(k - 1)
+
+            @pl.when(
+                jnp.logical_and(
+                    section == 0, jnp.logical_and(k > CHUNKS, (k - 1) % CHUNKS == 0)
+                )
+            )
+            def _():
+                weights((k - 1) // CHUNKS - 1)
 
         @pl.when(chained == 0)
         def _():
@@ -382,35 +521,50 @@
 
         return carry
 
-    lax.fori_loop(0, 2 * micro, stage, 0)
+    lax.fori_loop(0, steps + micro, stage, 0)
     for bits in range(1, peers):
         gain_copy(me, bits).start()
 
-    def finish(m, carry):
-        for kind in (0, 1):
-            for bits in range(2, peers, 2):
-                arriving_rows(kind, m, bits).wait_recv()
-                relayed_rows(kind, m, bits).start()
-        for kind in (0, 1):
-            for bits in range(1, peers):
-                col_copy(kind, m, flipped(me, bits, peers), bits).wait_recv()
-        for kind in (0, 1):
-            for bits in range(1, peers, 2):
-                arriving_rows(kind, m, bits).wait_recv()
-
-        def weight(j, inside):
-            vg_ref[:, tile_at(j)] += jnp.dot(
-                cols_all[0, m], rows_all[1, m, :, tile_at(j)], preferred_element_type=jnp.float32
-            )
-            og_ref[:, tile_at(j)] += jnp.dot(
-                cols_all[1, m], rows_all[0, m, :, tile_at(j)], preferred_element_type=jnp.float32
-            )
-            return inside
-
-        lax.fori_loop(0, narrow, weight, 0)
-        return carry
-
-    lax.fori_loop(0, micro, finish, 0)
+    @pl.when(section > 0)
+    def _():
+        relay_values()
+
+        def early(k, carry):
+            relay_grads(k)
+            return carry
+
+        lax.fori_loop(0, steps - 1, early, 0)
+
+        def heavy(m, carry):
+            weights(m)
+            return carry
+
+        lax.fori_loop(0, micro - 1, heavy, 0)
+
+    relay_grads(steps - 1)
+    last = micro - 1
+    for kind in (0, 1):
+        gather(kind, last)
+        mine = coordinate(me, far[kind])
+
+        def given(j, carry):
+            part_out[kind, j] = (
+                acc[kind, 1 - mine, :, tile_at(j)] + product(kind, last, 1 - mine, j)
+            ).astype(jnp.bfloat16)
+            part_copy(kind, j).start()
+            return carry
+
+        lax.fori_loop(0, narrow, given, 0)
+
+    for kind in (0, 1):
+        mine = coordinate(me, far[kind])
+
+        def kept(j, carry):
+            acc[kind, mine, :, tile_at(j)] += product(kind, last, mine, j)
+            return carry
+
+        lax.fori_loop(0, narrow, kept, 0)
+
     for bits in range(1, peers):
         gain_copy(flipped(me, bits, peers), bits).wait_recv()
     gained = gain_all[0]
@@ -418,22 +572,42 @@
         gained = gained + gain_all[owner]
     gg_ref[...] = gained
 
+    for kind, out_ref in ((0, vg_ref), (1, og_ref)):
+        mine = coordinate(me, far[kind])
+
+        def join(j, carry):
+            part_copy(kind, j).wait_recv()
+            out_ref[:, tile_at(j)] = acc[kind, mine, :, tile_at(j)] + part_in[kind, j].astype(
+                jnp.float32
+            )
+            return carry
+
+        lax.fori_loop(0, narrow, join, 0)
+
     def drain(m, carry):
         for kind in (0, 1):
-            for bits in range(1, peers):
-                col_copy(kind, m, me, bits).wait_send()
-            for bits in (1, *range(2, peers, 2)):
-                own_rows(kind, m, bits).wait_send()
-            for bits in range(2, peers, 2):
-                relayed_rows(kind, m, bits).wait_send()
-
-        @pl.when(section > 0)
-        def _():
-            down_copy(m, section - 1).wait_send()
-
+            for bits in ways(kind):
+                for b in range(2):
+                    col_copy(kind, m, me, bits, b).wait_send()
+            for h in range(CHUNKS if kind == 0 else 1):
+                own_to_core(kind, m, h).wait_send()
+                own_to_chip(kind, m, h).wait_send()
+                relay(kind, m, h).wait_send()
         return carry
 
     lax.fori_loop(0, micro, drain, 0)
+
+    @pl.when(section > 0)
+    def _():
+        def sent(k, carry):
+            down_copy(k, section - 1).wait_send()
+            return carry
+
+        lax.fori_loop(0, steps, sent, 0)
+
+    for kind in (0, 1):
+        for j in range(narrow):
+            part_copy(kind, j).wait_send()
     for bits in range(1, peers):
         gain_copy(me, bits).wait_send()
 
@@ -443,7 +617,10 @@
     micro, tokens, width = cotangent.shape
     inner = value_weight.shape[2]
     share = width // peers
-    hbm = pl.BlockSpec(memory_space=pltpu.VMEM)
+    narrow = inner // TILE
+    chunk = tokens // CHUNKS
+    held = pl.BlockSpec(memory_space=pltpu.VMEM)
+    far_off = pl.BlockSpec(memory_space=pl.ANY)
     value_grad, out_grad, gain_grad = pl.pallas_call(
         functools.partial(fused_kernel, peers, sections),
         out_shape=(
@@ -451,23 +628,40 @@
             jax.ShapeDtypeStruct((share, inner), jnp.float32),
             jax.ShapeDtypeStruct((1, width), jnp.float32),
         ),
-        in_specs=[pl.BlockSpec(memory_space=pltpu.SMEM)] + [hbm] * 5,
-        out_specs=(hbm, hbm, hbm),
+        in_specs=[
+            pl.BlockSpec(memory_space=pltpu.SMEM),
+            far_off,
+            far_off,
+            held,
+            far_off,
+            far_off,
+        ],
+        out_specs=(held, held, held),
         scratch_shapes=[
+            pltpu.VMEM((micro, tokens, width), jnp.bfloat16),
+            pltpu.VMEM((width, inner), jnp.bfloat16),
+            pltpu.VMEM((width, inner), jnp.bfloat16),
             pltpu.VMEM((micro, tokens, 1), jnp.float32),
             pltpu.VMEM((micro, tokens, width), jnp.bfloat16),
             pltpu.VMEM((micro, tokens, width), jnp.bfloat16),
-            (pltpu.VMEM((tokens, width), jnp.bfloat16), pltpu.VMEM((tokens, width), jnp.float32)),
-            pltpu.VMEM((2, micro, peers * tokens, inner), jnp.bfloat16),
+            pltpu.VMEM((tokens, width), jnp.bfloat16),
+            pltpu.VMEM((chunk, width), jnp.float32),
+            pltpu.VMEM((2, micro, 4 * tokens, inner), jnp.bfloat16),
             pltpu.VMEM((2, micro, width, tokens), jnp.bfloat16),
-            pltpu.VMEM((2, micro, share, peers * tokens), jnp.bfloat16),
+            pltpu.VMEM((2, micro, 2, share, 4 * tokens), jnp.bfloat16),
+            pltpu.VMEM((2, 2, share, inner), jnp.float32),
+            pltpu.VMEM((2, narrow, share, TILE), jnp.bfloat16),
+            pltpu.VMEM((2, narrow, share, TILE), jnp.bfloat16),
             pltpu.VMEM((peers, 1, width), jnp.float32),
-            pltpu.SemaphoreType.DMA((2, micro, peers)),
-            pltpu.SemaphoreType.DMA((2, micro, peers)),
-            pltpu.SemaphoreType.DMA((2, micro, peers)),
-            pltpu.SemaphoreType.DMA((2, micro, peers)),
-            pltpu.SemaphoreType.DMA((micro,)),
-            pltpu.SemaphoreType.DMA((micro,)),
+            pltpu.SemaphoreType.DMA((4,)),
+            pltpu.SemaphoreType.DMA((2, micro, CHUNKS, 3)),
+            pltpu.SemaphoreType.DMA((2, micro, CHUNKS, 3)),
+            pltpu.SemaphoreType.DMA((2, micro, peers, 2)),
+            pltpu.SemaphoreType.DMA((2, micro, peers, 2)),
+            pltpu.SemaphoreType.DMA((micro * CHUNKS,)),
+            pltpu.SemaphoreType.DMA((micro * CHUNKS,)),
+            pltpu.SemaphoreType.DMA((2, narrow)),
+            pltpu.SemaphoreType.DMA((2, narrow)),
             pltpu.SemaphoreType.DMA((peers,)),
             pltpu.SemaphoreType.DMA((peers,)),
         ],
@@ -482,10 +676,12 @@
     peers = mesh.shape["seq"]
     micro, tokens, width = cotangent.shape
     inner = value_weight.shape[2]
-    held = 4 * width * inner + 4 * micro * tokens * (2 * width + inner * peers)
-    held += 4 * micro * tokens * width * 3 + 8 * (width // peers) * inner + 6 * tokens * width
+    share = width // peers
+    held = 4 * width * inner + 2 * 2 * micro * 4 * tokens * (inner + 2 * share)
+    held += 2 * micro * tokens * width * 5 + 6 * tokens * width
+    held += share * inner * (4 * 4 + 4 * 2 + 4 * 2)
     return (
-        peers & (peers - 1) == 0
+        peers == 8
         and tokens % LANES == 0
         and width % TILE == 0
         and inner % TILE == 0

time: 136 us -> 124 us (0.912)
  Pallas kernels: 131 us -> 119 us
    pallas_call x1, Pallas kernels: 131 us -> 119 us  [fused(): pl.pallas_call(functools.partial(fused_kernel, peers, sections), out_shap...]
where the time goes in v1:
time: 124 us
  Pallas kernels  119 us (96%)
  local copies, waits for them, and re-layouts  4.12 us (3%)
    pallas_call x1, Pallas kernels, fused(): pl.pallas_call(functools.partial(fused_kernel, peers, sections), out_shap...  119 us
    unnamed x7, local copies, waits for them, and re-layouts  4.12 us

profile of v1, /device:TPU:0, one launch (start us, length us, event | category | flops | bytes accessed | tf_op | source)
XLA Modules:
  0.0 123.5 jit_solution(6538444745161520583)
XLA Ops:
  0.6 118.8 %shard_map.85 = (f32[288,1024]{1,0:T(8,128)}, f32[288,1024]{1,0:T(8,128)}, f32[1,2304]{1,0:T(1,128)}) custom-call(s32[1,3]{1,0:T(1,128)} %slot_ref.1, bf16[3,128,2304]{2,1,0:T(8,128)(2,1)} %bitcast.7, bf16[3,128,2304]{2,1,0:T(8,128)(2,1)} %cot_hbm.1, f32[1,2304]{1,0:T(1,128)} %gain_ref.1, bf16[2304,1024]{1,0:T(8,128)(2,1)} %bitcast.5, bf16[2304,1024]{1,0:T(8,128)(2,1)} %bitcast.6), custom_call_target="tpu_custom_call" | custom-call | tf_op jit(solution)/shard_map/pallas_call | solution.py:624
  119.4 0.0 copy-start
  119.4 2.5 %copy.12 = f32[1,288,1024]{2,1,0:T(8,128)} copy(f32[1,288,1024]{2,1,0:T(8,128)} %bitcast.9) | data formatting | bytes 2359296
  121.9 0.0 copy-done
  121.9 0.0 copy-start.1
  121.9 1.0 copy.13
  122.9 0.0 copy-done.1
  122.9 0.6 copy.14
Async XLA Ops:
  119.4 2.5 %copy-start = (f32[288,1024]{1,0:T(8,128)S(1)}, f32[288,1024]{1,0:T(8,128)}, u32[]{:S(2)}) copy-start(f32[288,1024]{1,0:T(8,128)} %get-tuple-element.7) | copy-start | bytes 3538948
  121.9 1.0 copy-start.1

commit v2 on v1

--- a/solution.py
+++ b/solution.py
@@ -152,6 +152,7 @@
     saved_ref,
     wv_ref,
     wo_ref,
+    wvt_ref,
     inv_buf,
     grad_buf,
     pass_buf,
@@ -163,8 +164,10 @@
     acc,
     part_out,
     part_in,
+    gain_part,
     gain_all,
     load_sem,
+    out_sem,
     rows_send,
     rows_recv,
     cols_send,
@@ -288,9 +291,13 @@
     @pl.when(top)
     def _():
         load_cot.start()
-
-    load_wo.start()
-    load_wv.start()
+        load_wo.start()
+        load_wv.start()
+
+    @pl.when(section < sections - 1)
+    def _():
+        load_wv.start()
+        load_wo.start()
 
     barrier = pltpu.get_barrier_semaphore()
     for bits in range(1, peers):
@@ -316,17 +323,17 @@
             device_id_type=pl.DeviceIdType.MESH,
         )
 
-    gain_all[me] = jnp.zeros((1, width), jnp.float32)
+    gain_part[...] = jnp.zeros_like(gain_part)
     load_saved.wait()
 
     def scales(m, carry):
         slot = slot_ref[0, m]
 
-        def squares(j, total):
-            x = saved_ref[slot, :, tile_at(j)].astype(jnp.float32)
-            return total + jnp.sum(x * x, axis=1, keepdims=True)
-
-        total = lax.fori_loop(0, wide, squares, jnp.zeros((tokens, 1), jnp.float32))
+        total = jnp.zeros((tokens, LANES), jnp.float32)
+        for j in range(width // LANES):
+            x = saved_ref[slot, :, j * LANES : (j + 1) * LANES].astype(jnp.float32)
+            total = total + x * x
+        total = jnp.sum(total, axis=1, keepdims=True)
         inv_buf[m] = lax.rsqrt(total / width + EPSILON)
         return carry
 
@@ -336,8 +343,11 @@
     def _():
         load_cot.wait()
 
+    @pl.when(section < sections - 1)
+    def _():
+        load_wv.wait()
+
     load_wo.wait()
-    load_wv.wait()
     pl.semaphore_wait(
         barrier,
         peers - 1
@@ -358,32 +368,23 @@
         slot = slot_ref[0, m]
         inv = inv_buf[m]
 
-        def norm(j, carry):
-            x = saved_ref[slot, :, tile_at(j)].astype(jnp.float32)
-            n = (x * inv * gain_ref[:, tile_at(j)]).astype(jnp.bfloat16)
-            normed[:, tile_at(j)] = n
-            turned[0, m, tile_at(j)] = n.T
-            return carry
-
-        lax.fori_loop(0, wide, norm, 0)
+        for j in range(wide):
+            cols = slice(j * TILE, (j + 1) * TILE)
+            x = saved_ref[slot, :, cols].astype(jnp.float32)
+            n = (x * inv * gain_ref[:, cols]).astype(jnp.bfloat16)
+            normed[:, cols] = n
+            turned[0, m, cols] = n.T
         send_cols(0, m)
-
-        def project(j, carry):
-            rows_all[1, m, tile_at(place(1, me), tokens), tile_at(j)] = jnp.dot(
-                normed[...], wv_ref[:, tile_at(j)], preferred_element_type=jnp.float32
-            ).astype(jnp.bfloat16)
-            return carry
-
-        lax.fori_loop(0, narrow, project, 0)
+        rows_all[1, m, tile_at(place(1, me), tokens)] = jnp.dot(
+            normed[...], wv_ref[...], preferred_element_type=jnp.float32
+        ).astype(jnp.bfloat16)
         own_to_chip(1, m, 0).start()
         own_to_core(1, m, 0).start()
 
     def turn(m):
-        def tile(j, carry):
-            turned[1, m, tile_at(j)] = grad_buf[m, :, tile_at(j)].T
-            return carry
-
-        lax.fori_loop(0, wide, tile, 0)
+        for j in range(wide):
+            cols = slice(j * TILE, (j + 1) * TILE)
+            turned[1, m, cols] = grad_buf[m, :, cols].T
         send_cols(1, m)
 
     def chain(k):
@@ -397,49 +398,69 @@
         def _():
             down_copy(k, section + 1).wait_recv()
 
-        def project(j, carry):
-            rows_all[0, m, mine, tile_at(j)] = jnp.dot(
-                grad_buf[m, here], wo_ref[:, tile_at(j)], preferred_element_type=jnp.float32
-            ).astype(jnp.bfloat16)
-            return carry
-
-        lax.fori_loop(0, narrow, project, 0)
-        own_to_chip(0, m, h).start()
-        own_to_core(0, m, h).start()
-
         @pl.when(jnp.logical_and(section == 0, h == CHUNKS - 1))
         def _():
             turn(m)
 
-        def back(j, total):
-            term = lax.dot_general(
-                rows_all[0, m, mine],
-                wv_ref[tile_at(j)],
-                (((1,), (1,)), ((), ())),
-                preferred_element_type=jnp.float32,
-            )
-            unit = saved_ref[slot, here, tile_at(j)].astype(jnp.float32) * inv
-            gn[:, tile_at(j)] = term
-            both = term * unit
-            gain_all[me, :, tile_at(j)] += jnp.sum(both, axis=0, keepdims=True)
-            return total + jnp.sum(both * gain_ref[:, tile_at(j)], axis=1, keepdims=True)
-
-        total = lax.fori_loop(0, wide, back, jnp.zeros((chunk, 1), jnp.float32))
-        mean = total / width
-
-        @pl.when(section > 0)
+        rows_all[0, m, mine] = jnp.dot(
+            grad_buf[m, here], wo_ref[...], preferred_element_type=jnp.float32
+        ).astype(jnp.bfloat16)
+        own_to_chip(0, m, h).start()
+        own_to_core(0, m, h).start()
+
+        def back(flip):
+            grad_value = rows_all[0, m, mine]
+            total = jnp.zeros((chunk, LANES), jnp.float32)
+            for j in range(wide // 3):
+                cols = slice(j * 3 * TILE, (j + 1) * 3 * TILE)
+                if flip:
+                    term = lax.dot_general(
+                        grad_value,
+                        wv_ref[cols],
+                        (((1,), (1,)), ((), ())),
+                        preferred_element_type=jnp.float32,
+                    )
+                else:
+                    term = jnp.dot(
+                        grad_value, wvt_ref[:, cols], preferred_element_type=jnp.float32
+                    )
+                unit = saved_ref[slot, here, cols].astype(jnp.float32) * inv
+                grad_unit = term * gain_ref[:, cols]
+                gn[:, cols] = grad_unit
+                gain_part[:, cols] += jnp.sum(
+                    (term * unit).reshape(chunk // 8, 8, 3 * TILE), axis=0
+                )
+                both = grad_unit * unit
+                for i in range(3 * TILE // LANES):
+                    total = total + both[:, i * LANES : (i + 1) * LANES]
+            return jnp.sum(total, axis=1, keepdims=True) / width
+
+        def down(mean):
+            pull = inv * inv * mean
+            for j in range(wide):
+                cols = slice(j * TILE, (j + 1) * TILE)
+                pass_buf[m, here, cols] = (
+                    grad_buf[m, here, cols].astype(jnp.float32)
+                    + inv * gn[:, cols]
+                    - saved_ref[slot, here, cols].astype(jnp.float32) * pull
+                ).astype(jnp.bfloat16)
+            down_copy(k, section - 1).start()
+
+        @pl.when(top)
         def _():
-            def step(j, carry):
-                unit = saved_ref[slot, here, tile_at(j)].astype(jnp.float32) * inv
-                grad_unit = gn[:, tile_at(j)] * gain_ref[:, tile_at(j)]
-                pass_buf[m, here, tile_at(j)] = (
-                    grad_buf[m, here, tile_at(j)].astype(jnp.float32)
-                    + inv * (grad_unit - unit * mean)
-                ).astype(jnp.bfloat16)
-                return carry
-
-            lax.fori_loop(0, wide, step, 0)
-            down_copy(k, section - 1).start()
+            @pl.when(k == 0)
+            def _():
+                load_wv.wait()
+
+            down(back(True))
+
+        @pl.when(section < sections - 1)
+        def _():
+            mean = back(False)
+
+            @pl.when(section > 0)
+            def _():
+                down(mean)
 
         @pl.when(jnp.logical_and(section > 0, h == CHUNKS - 1))
         def _():
@@ -465,27 +486,29 @@
             from_core(kind, m, h).wait_recv()
             from_relay(kind, m, h).wait_recv()
 
-    def product(kind, m, b, j):
+    def product(kind, m, b, cols):
         return jnp.dot(
             cols_all[kind, m, b],
-            rows_all[kind, m, :, tile_at(j)],
+            rows_all[kind, m, :, cols],
             preferred_element_type=jnp.float32,
         )
 
     def weights(m):
         for kind in (0, 1):
             gather(kind, m)
-
-            def tile(i, carry):
-                b, j = i // narrow, i % narrow
-                acc[kind, b, :, tile_at(j)] += product(kind, m, b, j)
-                return carry
-
-            lax.fori_loop(0, 2 * narrow, tile, 0)
-
-    @pl.when(section > 0)
-    def _():
-        acc[...] = jnp.zeros_like(acc)
+            both = cols_all[kind, m].reshape(2 * share, 4 * tokens)
+            for j in range(inner // (2 * TILE)):
+                cols = slice(j * 2 * TILE, (j + 1) * 2 * TILE)
+                acc[kind, :, :, cols] += jnp.dot(
+                    both, rows_all[kind, m, :, cols], preferred_element_type=jnp.float32
+                ).reshape(2, share, 2 * TILE)
+
+    def transpose_weights():
+        def tile(j, carry):
+            wvt_ref[:, tile_at(j)] = wv_ref[tile_at(j)].T
+            return carry
+
+        lax.fori_loop(0, wide, tile, 0)
 
     def stage(t, carry):
         at_top = top.astype(jnp.int32)
@@ -496,6 +519,10 @@
 
         @pl.when(chained == 1)
         def _():
+            @pl.when(jnp.logical_and(section < sections - 1, k == 0))
+            def _():
+                transpose_weights()
+
             @pl.when(jnp.logical_and(section == 0, k == 0))
             def _():
                 acc[...] = jnp.zeros_like(acc)
@@ -522,11 +549,13 @@
         return carry
 
     lax.fori_loop(0, steps + micro, stage, 0)
+    gain_all[me] = jnp.sum(gain_part[...], axis=0, keepdims=True)
     for bits in range(1, peers):
         gain_copy(me, bits).start()
 
     @pl.when(section > 0)
     def _():
+        acc[...] = jnp.zeros_like(acc)
         relay_values()
 
         def early(k, carry):
@@ -547,23 +576,18 @@
         gather(kind, last)
         mine = coordinate(me, far[kind])
 
-        def given(j, carry):
+        for j in range(narrow):
+            cols = slice(j * TILE, (j + 1) * TILE)
             part_out[kind, j] = (
-                acc[kind, 1 - mine, :, tile_at(j)] + product(kind, last, 1 - mine, j)
+                acc[kind, 1 - mine, :, cols] + product(kind, last, 1 - mine, cols)
             ).astype(jnp.bfloat16)
             part_copy(kind, j).start()
-            return carry
-
-        lax.fori_loop(0, narrow, given, 0)
 
     for kind in (0, 1):
         mine = coordinate(me, far[kind])
-
-        def kept(j, carry):
-            acc[kind, mine, :, tile_at(j)] += product(kind, last, mine, j)
-            return carry
-
-        lax.fori_loop(0, narrow, kept, 0)
+        for j in range(narrow):
+            cols = slice(j * TILE, (j + 1) * TILE)
+            acc[kind, mine, :, cols] += product(kind, last, mine, cols)
 
     for bits in range(1, peers):
         gain_copy(flipped(me, bits, peers), bits).wait_recv()
@@ -572,17 +596,20 @@
         gained = gained + gain_all[owner]
     gg_ref[...] = gained
 
-    for kind, out_ref in ((0, vg_ref), (1, og_ref)):
+    def out_copy(kind, j):
+        return pltpu.make_async_copy(
+            acc.at[kind, coordinate(me, far[kind]), :, tile_at(j)],
+            (vg_ref, og_ref)[kind].at[:, tile_at(j)],
+            out_sem.at[kind, j],
+        )
+
+    for kind in (0, 1):
         mine = coordinate(me, far[kind])
-
-        def join(j, carry):
+        for j in range(narrow):
+            cols = slice(j * TILE, (j + 1) * TILE)
             part_copy(kind, j).wait_recv()
-            out_ref[:, tile_at(j)] = acc[kind, mine, :, tile_at(j)] + part_in[kind, j].astype(
-                jnp.float32
-            )
-            return carry
-
-        lax.fori_loop(0, narrow, join, 0)
+            acc[kind, mine, :, cols] += part_in[kind, j].astype(jnp.float32)
+            out_copy(kind, j).start()
 
     def drain(m, carry):
         for kind in (0, 1):
@@ -608,6 +635,7 @@
     for kind in (0, 1):
         for j in range(narrow):
             part_copy(kind, j).wait_send()
+            out_copy(kind, j).wait()
     for bits in range(1, peers):
         gain_copy(me, bits).wait_send()
 
@@ -636,11 +664,12 @@
             far_off,
             far_off,
         ],
-        out_specs=(held, held, held),
+        out_specs=(far_off, far_off, held),
         scratch_shapes=[
             pltpu.VMEM((micro, tokens, width), jnp.bfloat16),
             pltpu.VMEM((width, inner), jnp.bfloat16),
             pltpu.VMEM((width, inner), jnp.bfloat16),
+            pltpu.VMEM((inner, width), jnp.bfloat16),
             pltpu.VMEM((micro, tokens, 1), jnp.float32),
             pltpu.VMEM((micro, tokens, width), jnp.bfloat16),
             pltpu.VMEM((micro, tokens, width), jnp.bfloat16),
@@ -652,8 +681,10 @@
             pltpu.VMEM((2, 2, share, inner), jnp.float32),
             pltpu.VMEM((2, narrow, share, TILE), jnp.bfloat16),
             pltpu.VMEM((2, narrow, share, TILE), jnp.bfloat16),
+            pltpu.VMEM((8, width), jnp.float32),
             pltpu.VMEM((peers, 1, width), jnp.float32),
             pltpu.SemaphoreType.DMA((4,)),
+            pltpu.SemaphoreType.DMA((2, narrow)),
             pltpu.SemaphoreType.DMA((2, micro, CHUNKS, 3)),
             pltpu.SemaphoreType.DMA((2, micro, CHUNKS, 3)),
             pltpu.SemaphoreType.DMA((2, micro, peers, 2)),
@@ -677,14 +708,14 @@
     micro, tokens, width = cotangent.shape
     inner = value_weight.shape[2]
     share = width // peers
-    held = 4 * width * inner + 2 * 2 * micro * 4 * tokens * (inner + 2 * share)
+    held = 6 * width * inner + 2 * 2 * micro * 4 * tokens * (inner + 2 * share)
     held += 2 * micro * tokens * width * 5 + 6 * tokens * width
     held += share * inner * (4 * 4 + 4 * 2 + 4 * 2)
     return (
         peers == 8
         and tokens % LANES == 0
-        and width % TILE == 0
-        and inner % TILE == 0
+        and width % (3 * TILE) == 0
+        and inner % (2 * TILE) == 0
         and width % (16 * peers) == 0
         and held < VMEM_BYTES - 4 * 1024 * 1024
     )

time: 124 us -> 99.5 us (0.80)
  Pallas kernels: 119 us -> 94.6 us
    pallas_call x1, Pallas kernels: 119 us -> 94.6 us  [fused(): pl.pallas_call(functools.partial(fused_kernel, peers, sections), out_shap...]
where the time goes in v2:
time: 99.5 us; the launch traced here: 99.3 us
  Pallas kernels  94.6 us (95%)
  local copies, waits for them, and re-layouts  4.12 us (4%)
    pallas_call x1, Pallas kernels, fused(): pl.pallas_call(functools.partial(fused_kernel, peers, sections), out_shap...  94.6 us
    unnamed x7, local copies, waits for them, and re-layouts  4.12 us

profile of v2, /device:TPU:0, one launch (start us, length us, event | category | flops | bytes accessed | tf_op | source)
XLA Modules:
  0.0 99.3 jit_solution(5019335712891837385)
XLA Ops:
  0.6 94.6 %shard_map.85 = (f32[288,1024]{1,0:T(8,128)}, f32[288,1024]{1,0:T(8,128)}, f32[1,2304]{1,0:T(1,128)}) custom-call(s32[1,3]{1,0:T(1,128)} %slot_ref.1, bf16[3,128,2304]{2,1,0:T(8,128)(2,1)} %bitcast.7, bf16[3,128,2304]{2,1,0:T(8,128)(2,1)} %cot_hbm.1, f32[1,2304]{1,0:T(1,128)} %gain_ref.1, bf16[2304,1024]{1,0:T(8,128)(2,1)} %bitcast.5, bf16[2304,1024]{1,0:T(8,128)(2,1)} %bitcast.6), custom_call_target="tpu_custom_call" | custom-call | tf_op jit(solution)/shard_map/pallas_call | solution.py:652
  95.2 0.0 copy-start
  95.2 2.5 %copy.12 = f32[1,288,1024]{2,1,0:T(8,128)} copy(f32[1,288,1024]{2,1,0:T(8,128)} %bitcast.9) | data formatting | bytes 2359296
  97.7 0.0 copy-done
  97.7 0.0 copy-start.1
  97.7 1.0 %copy.13 = f32[1,288,1024]{2,1,0:T(8,128)} copy(f32[1,288,1024]{2,1,0:T(8,128)S(1)} %bitcast.8) | data formatting | bytes 2359296
  98.7 0.0 copy-done.1
  98.7 0.6 copy.14
Async XLA Ops:
  95.2 2.5 %copy-start = (f32[288,1024]{1,0:T(8,128)S(1)}, f32[288,1024]{1,0:T(8,128)}, u32[]{:S(2)}) copy-start(f32[288,1024]{1,0:T(8,128)} %get-tuple-element.7) | copy-start | bytes 3538948
  97.7 1.0 %copy-start.1 = (f32[1,2304]{1,0:T(1,128)S(1)}, f32[1,2304]{1,0:T(1,128)}, u32[]{:S(2)}) copy-start(f32[1,2304]{1,0:T(1,128)} %get-tuple-element.14) | copy-start | bytes 27652

commit v3 on v2

v3 whole, which is shorter than its diff:
```python
import functools

import jax
import jax.numpy as jnp
from jax import lax
from jax.experimental import pallas as pl
from jax.experimental.pallas import tpu as pltpu
from jax.sharding import PartitionSpec as P

EPSILON = 1e-06


def passed_along(value, axis, steps):
    count = lax.axis_size(axis)
    first, last = (max(0, -steps), min(count, count - steps))
    return lax.ppermute(value, axis, [(source, source + steps) for source in range(first, last)])


def normalize(inputs, gain_row):
    value_rows = inputs.astype(jnp.float32)
    inv_rms = lax.rsqrt(jnp.mean(value_rows * value_rows, axis=-1, keepdims=True) + EPSILON)
    unit_rows = value_rows * inv_rms
    return (unit_rows, inv_rms, (unit_rows * gain_row).astype(jnp.bfloat16))


def input_grads(inputs, grad_out, gain_row, w_value, w_out):
    unit_rows, inv_rms, normed = normalize(inputs, gain_row)
    grad_value = jnp.dot(grad_out, w_out, preferred_element_type=jnp.float32).astype(jnp.bfloat16)
    grad_normed = lax.dot_general(
        grad_value, w_value, (((1,), (1,)), ((), ())), preferred_element_type=jnp.float32
    )
    gain_term = jnp.sum(grad_normed * unit_rows, axis=0)
    grad_unit = grad_normed * gain_row
    grad_in = grad_out.astype(jnp.float32) + inv_rms * (
        grad_unit - unit_rows * jnp.mean(grad_unit * unit_rows, axis=-1, keepdims=True)
    )
    return (grad_in.astype(jnp.bfloat16), grad_value, normed, gain_term)


def arrivals(
    step_index, sent, section_count, section_index, micro_count, cotangent, local_saved, slot_order
):
    if step_index > 0:
        incoming = passed_along(sent, "section", -1)
    else:
        incoming = sent
    micro_index = step_index - (section_count - 1 - section_index)
    active_now = jnp.logical_and(micro_index >= 0, micro_index < micro_count)
    clipped = jnp.clip(micro_index, 0, micro_count - 1)
    top_grad = lax.dynamic_index_in_dim(cotangent, clipped, 0, keepdims=False)
    grad_out = jnp.where(section_index == section_count - 1, top_grad, incoming)
    slot_index = lax.dynamic_index_in_dim(slot_order, clipped, 0, keepdims=False)
    inputs = lax.dynamic_index_in_dim(local_saved, slot_index, 0, keepdims=False)
    return (active_now, clipped, grad_out, inputs)


def per_device(saved, cotangent, slot_table, gain, value_weight, out_weight):
    section_count = lax.axis_size("section")
    section_index = lax.axis_index("section")
    micro_count = slot_table.shape[1]
    local_saved = saved[0]
    slot_order = slot_table[0]
    gain_row = gain[0]
    w_value = value_weight[0]
    w_out = out_weight[0]
    token_rows = cotangent.shape[1]
    model_width = w_value.shape[0]
    inner_width = w_value.shape[1]
    sent = jnp.zeros((token_rows, model_width), jnp.bfloat16)
    gain_acc = jnp.zeros((model_width,), jnp.float32)
    out_stash = jnp.zeros((micro_count, token_rows, model_width), jnp.bfloat16)
    value_stash = jnp.zeros((micro_count, token_rows, inner_width), jnp.bfloat16)
    for step_index in range(micro_count + section_count - 1):
        active_now, clipped, grad_out, inputs = arrivals(
            step_index,
            sent,
            section_count,
            section_index,
            micro_count,
            cotangent,
            local_saved,
            slot_order,
        )

        def working(carried):
            grad_in, grad_value, normed, gain_term = input_grads(
                inputs, grad_out, gain_row, w_value, w_out
            )
            new_out = lax.dynamic_update_index_in_dim(carried[2], grad_out, clipped, 0)
            new_value = lax.dynamic_update_index_in_dim(carried[3], grad_value, clipped, 0)
            return (grad_in, carried[1] + gain_term, new_out, new_value)

        def resting(carried):
            return carried

        sent, gain_acc, out_stash, value_stash = lax.cond(
            active_now, working, resting, (sent, gain_acc, out_stash, value_stash)
        )
    ordered = jnp.take(local_saved, slot_order, axis=0).reshape(
        micro_count * token_rows, model_width
    )
    unit_all, inv_all, normed_all = normalize(ordered, gain_row)
    values_all = jnp.dot(normed_all, w_value, preferred_element_type=jnp.float32).astype(
        jnp.bfloat16
    )
    grads_all = out_stash.reshape(micro_count * token_rows, model_width)
    grad_values = value_stash.reshape(micro_count * token_rows, inner_width)
    value_acc = lax.dot_general(
        normed_all, grad_values, (((0,), (0,)), ((), ())), preferred_element_type=jnp.float32
    )
    out_acc = lax.dot_general(
        grads_all, values_all, (((0,), (0,)), ((), ())), preferred_element_type=jnp.float32
    )
    value_grad, out_grad = (
        lax.psum_scatter(value_acc, "seq", scatter_dimension=0, tiled=True),
        lax.psum_scatter(out_acc, "seq", scatter_dimension=0, tiled=True),
    )
    gain_total = lax.psum(gain_acc, "seq")
    return (value_grad[None], out_grad[None], gain_total[None])


TILE = 256
LANES = 128
CHUNKS = 4
VMEM_BYTES = 50 * 1024 * 1024


def flipped(index, bits, count):
    total, unit = 0, 1
    while unit < count:
        total = total + ((index // unit + (bits // unit) % 2) % 2) * unit
        unit *= 2
    return total


def tile_at(index, size=TILE):
    return pl.ds(pl.multiple_of(index * size, size), size)


def fused_kernel(
    peers,
    sections,
    slot_ref,
    saved_hbm,
    cot_hbm,
    gain_ref,
    wv_hbm,
    wo_hbm,
    vg_ref,
    og_ref,
    gg_ref,
    saved_ref,
    wv_ref,
    wo_ref,
    wvt_ref,
    inv_buf,
    grad_buf,
    pass_buf,
    normed,
    gn,
    rows_gv,
    rows_v,
    turned,
    cols_all,
    acc,
    part_out,
    part_in,
    gain_part,
    gain_all,
    load_sem,
    wv_sem,
    gv_send,
    gv_chip,
    gv_pair,
    v_send,
    v_chip,
    v_pair,
    cols_send,
    cols_recv,
    down_send,
    down_recv,
    part_send,
    part_recv,
    gain_send,
    gain_recv,
):
    section = lax.axis_index("section")
    me = lax.axis_index("seq")
    micro, tokens, width = grad_buf.shape
    inner = wv_ref.shape[1]
    share = width // peers
    wide, narrow = width // TILE, inner // TILE
    third = width // 3
    chunk, half = tokens // CHUNKS, tokens // 2
    steps = micro * CHUNKS
    top = section == sections - 1
    near = (peers // 4, peers // 2)
    far = (peers // 2, peers // 4)

    def peer(bits):
        return {"seq": flipped(me, bits, peers)}

    def coordinate(device, bit):
        return (device // bit) % 2

    def place(kind, device):
        return coordinate(device, near[kind]) * 2 + device % 2

    def remote(source, target, send_sem, recv_sem, device):
        return pltpu.make_async_remote_copy(
            src_ref=source,
            dst_ref=target,
            send_sem=send_sem,
            recv_sem=recv_sem,
            device_id=device,
            device_id_type=pl.DeviceIdType.MESH,
        )

    def gv_copy(k, owner, recv_sem, bits):
        m, h = k // CHUNKS, k % CHUNKS
        spot = rows_gv.at[m, tile_at(place(0, owner) * CHUNKS + h, chunk)]
        return remote(spot, spot, gv_send.at[0], recv_sem, peer(bits))

    def gv_to_chip(k):
        return gv_copy(k, me, gv_chip.at[k], near[0])

    def gv_from_chip(k):
        return gv_copy(k, flipped(me, near[0], peers), gv_chip.at[k], near[0])

    def gv_to_core(k):
        return gv_copy(k, me, gv_pair.at[k // CHUNKS], 1)

    def gv_relay(k):
        return gv_copy(k, flipped(me, near[0], peers), gv_pair.at[k // CHUNKS], 1)

    def gv_pairs(m):
        spot = rows_gv.at[m, : 2 * tokens]
        return remote(spot, spot, gv_send.at[0], gv_pair.at[m], peer(1))

    def gv_all():
        spot = rows_gv.at[:, : 3 * tokens]
        return remote(spot, spot, gv_send.at[0], gv_pair.at[0], peer(1))

    def v_copy(m, owner, recv_sem, bits):
        spot = rows_v.at[m, :, tile_at(place(1, owner), half)]
        return remote(spot, spot, v_send.at[0], recv_sem, peer(bits))

    def v_to_chip(m):
        return v_copy(m, me, v_chip.at[m], near[1])

    def v_from_chip(m):
        return v_copy(m, flipped(me, near[1], peers), v_chip.at[m], near[1])

    def v_to_core(m):
        return v_copy(m, me, v_pair.at[m], 1)

    def v_relay(m):
        return v_copy(m, flipped(me, near[1], peers), v_pair.at[m], 1)

    def v_pairs(m):
        spot = rows_v.at[m, :, : 2 * half]
        return remote(spot, spot, v_send.at[0], v_pair.at[m], peer(1))

    def v_all():
        spot = rows_v.at[:, :, : 3 * half]
        return remote(spot, spot, v_send.at[0], v_pair.at[0], peer(1))

    def ways(kind):
        return (near[kind], near[kind] + 1, 1)

    def col_source(kind, m, part, target):
        if kind == 0:
            block = target + (part - coordinate(target, far[0])) * far[0]
        else:
            block = part * 4 + place(1, target)
        return turned.at[kind, m, tile_at(block, share)]

    def col_copy(kind, m, part, bits):
        return remote(
            col_source(kind, m, part, flipped(me, bits, peers)),
            cols_all.at[kind, m, part, :, tile_at(place(kind, me), tokens)],
            cols_send.at[kind],
            cols_recv.at[kind, m, part if kind == 1 else 0],
            peer(bits),
        )

    def send_cols(kind, m, parts):
        for bits in ways(kind):
            for part in parts:
                col_copy(kind, m, part, bits).start()
        for part in parts:
            cols_all[kind, m, part, :, tile_at(place(kind, me), tokens)] = col_source(
                kind, m, part, me
            )[...]

    def value_cols(m):
        spot = cols_all.at[0, m, :, :, : 3 * tokens]
        return remote(spot, spot, cols_send.at[0], cols_recv.at[0, m, 0], peer(1))

    def grad_cols(m, p):
        spot = cols_all.at[1, m, p, :, : 3 * tokens]
        return remote(spot, spot, cols_send.at[1], cols_recv.at[1, m, p], peer(1))

    def cols_sent(kind):
        spot = cols_all.at[kind, :, :, :, : 3 * tokens]
        return remote(spot, spot, cols_send.at[kind], cols_recv.at[kind, 0, 0], peer(1))

    def down_copy(k, target):
        spot = tile_at(k % CHUNKS, chunk)
        return remote(
            pass_buf.at[k // CHUNKS, spot],
            grad_buf.at[k // CHUNKS, spot],
            down_send.at[0],
            down_recv.at[k],
            {"section": target},
        )

    def part_copy(kind, j):
        return remote(
            part_out.at[kind, j],
            part_in.at[kind, j],
            part_send.at[kind],
            part_recv.at[kind, j],
            peer(far[kind]),
        )

    def gain_copy(bits):
        spot = gain_all.at[me]
        return remote(spot, spot, gain_send.at[0], gain_recv.at[0], peer(bits))

    def gains():
        spot = gain_all.at[: peers - 1]
        return remote(spot, spot, gain_send.at[0], gain_recv.at[0], peer(1))

    load_saved = pltpu.make_async_copy(saved_hbm, saved_ref, load_sem.at[0])
    load_wo = pltpu.make_async_copy(wo_hbm, wo_ref, load_sem.at[1])
    load_first = pltpu.make_async_copy(cot_hbm.at[0], grad_buf.at[0], load_sem.at[2])
    load_rest = pltpu.make_async_copy(cot_hbm.at[1:], grad_buf.at[1:], load_sem.at[3])

    def load_wv(j):
        rows = slice(j * third, (j + 1) * third)
        return pltpu.make_async_copy(wv_hbm.at[rows], wv_ref.at[rows], wv_sem.at[j])

    load_saved.start()

    @pl.when(top)
    def _():
        load_first.start()
        load_wo.start()
        for j in range(3):
            load_wv(j).start()
        load_rest.start()

    @pl.when(section < sections - 1)
    def _():
        for j in range(3):
            load_wv(j).start()
        load_wo.start()

    barrier = pltpu.get_barrier_semaphore()
    for bits in range(1, peers):
        pl.semaphore_signal(
            barrier, inc=1, device_id=peer(bits), device_id_type=pl.DeviceIdType.MESH
        )

    @pl.when(section > 0)
    def _():
        pl.semaphore_signal(
            barrier,
            inc=1,
            device_id={"section": section - 1},
            device_id_type=pl.DeviceIdType.MESH,
        )

    @pl.when(section < sections - 1)
    def _():
        pl.semaphore_signal(
            barrier,
            inc=1,
            device_id={"section": section + 1},
            device_id_type=pl.DeviceIdType.MESH,
        )

    gain_part[...] = jnp.zeros_like(gain_part)
    load_saved.wait()

    def scales(m, carry):
        slot = slot_ref[0, m]
        total = jnp.zeros((tokens, LANES), jnp.float32)
        for j in range(width // LANES):
            x = saved_ref[slot, :, j * LANES : (j + 1) * LANES].astype(jnp.float32)
            total = total + x * x
        total = jnp.sum(total, axis=1, keepdims=True)
        inv_buf[m] = lax.rsqrt(total / width + EPSILON)
        return carry

    lax.fori_loop(0, micro, scales, 0)

    pl.semaphore_wait(
        barrier,
        peers - 1
        + (section > 0).astype(jnp.int32)
        + (section < sections - 1).astype(jnp.int32),
    )

    @pl.when(top)
    def _():
        load_first.wait()
        load_wo.wait()

    @pl.when(section < sections - 1)
    def _():
        for j in range(3):
            load_wv(j).wait()

    def values(m):
        slot = slot_ref[0, m]
        inv = inv_buf[m]
        for j in range(wide):
            cols = slice(j * TILE, (j + 1) * TILE)
            x = saved_ref[slot, :, cols].astype(jnp.float32)
            n = (x * inv * gain_ref[:, cols]).astype(jnp.bfloat16)
            normed[:, cols] = n
            turned[0, m, cols] = n.T
        send_cols(0, m, (0, 1))
        result = jnp.dot(
            normed[...], wv_ref[...], preferred_element_type=jnp.float32
        ).astype(jnp.bfloat16)
        for p in range(2):
            rows_v[m, p, tile_at(place(1, me), half)] = result[p * half : (p + 1) * half]
        v_to_chip(m).start()
        v_to_core(m).start()

    def turn(m, p):
        block = width // 4
        for y in range(2):
            left, right = (
                grad_buf[m, tile_at(p, half), :].T[(2 * y + i) * block : (2 * y + i + 1) * block]
                for i in range(2)
            )
            turned[1, m, tile_at(p * 2 + y, block)] = jnp.concatenate([left, right], axis=1)

        @pl.when(p == 0)
        def _():
            send_cols(1, m, (0,))

        @pl.when(p == 1)
        def _():
            send_cols(1, m, (1,))

    def chain(k):
        m, h = k // CHUNKS, k % CHUNKS
        here = tile_at(h, chunk)
        slot = slot_ref[0, m]
        inv = inv_buf[m, here]
        mine = tile_at(place(0, me) * CHUNKS + h, chunk)
        turning = (h % (CHUNKS // 2)) == CHUNKS // 2 - 1

        @pl.when(section < sections - 1)
        def _():
            down_copy(k, section + 1).wait_recv()

        @pl.when(jnp.logical_and(section == 0, turning))
        def _():
            turn(m, h // (CHUNKS // 2))

        rows_gv[m, mine] = jnp.dot(
            grad_buf[m, here], wo_ref[...], preferred_element_type=jnp.float32
        ).astype(jnp.bfloat16)
        gv_to_chip(k).start()
        gv_to_core(k).start()

        def back(flip, first):
            grad_value = rows_gv[m, mine]
            total = jnp.zeros((chunk, LANES), jnp.float32)
            for j in range(3):
                cols = slice(j * third, (j + 1) * third)
                if flip:
                    if first:
                        load_wv(j).wait()
                    term = lax.dot_general(
                        grad_value,
                        wv_ref[cols],
                        (((1,), (1,)), ((), ())),
                        preferred_element_type=jnp.float32,
                    )
                else:
                    term = jnp.dot(
                        grad_value, wvt_ref[:, cols], preferred_element_type=jnp.float32
                    )
                unit = saved_ref[slot, here, cols].astype(jnp.float32) * inv
                grad_unit = term * gain_ref[:, cols]
                gn[:, cols] = grad_unit
                gain_part[:, cols] += jnp.sum(
                    (term * unit).reshape(chunk // 8, 8, third), axis=0
                )
                both = grad_unit * unit
                for i in range(third // LANES):
                    total = total + both[:, i * LANES : (i + 1) * LANES]
            return jnp.sum(total, axis=1, keepdims=True) / width

        def down(mean):
            pull = inv * inv * mean
            for j in range(wide):
                cols = slice(j * TILE, (j + 1) * TILE)
                pass_buf[m, here, cols] = (
                    grad_buf[m, here, cols].astype(jnp.float32)
                    + inv * gn[:, cols]
                    - saved_ref[slot, here, cols].astype(jnp.float32) * pull
                ).astype(jnp.bfloat16)
            down_copy(k, section - 1).start()

        @pl.when(jnp.logical_and(top, k == 0))
        def _():
            down(back(True, True))
            load_rest.wait()

        @pl.when(jnp.logical_and(top, k > 0))
        def _():
            down(back(True, False))

        @pl.when(section < sections - 1)
        def _():
            mean = back(False, False)

            @pl.when(section > 0)
            def _():
                down(mean)

        @pl.when(jnp.logical_and(section > 0, turning))
        def _():
            turn(m, h // (CHUNKS // 2))

    def relay_values():
        def one(m, carry):
            v_from_chip(m).wait_recv()
            v_relay(m).start()
            return carry

        lax.fori_loop(0, micro, one, 0)

    def relay_grads(k):
        gv_from_chip(k).wait_recv()
        gv_relay(k).start()

    def value_product(m):
        value_cols(m).wait_recv()
        gv_pairs(m).wait_recv()
        both = cols_all[0, m].reshape(2 * share, 4 * tokens)
        for j in range(inner // (2 * TILE)):
            cols = slice(j * 2 * TILE, (j + 1) * 2 * TILE)
            acc[0, :, :, cols] += jnp.dot(
                both, rows_gv[m, :, cols], preferred_element_type=jnp.float32
            ).reshape(2, share, 2 * TILE)

    def grad_lanes(m, p):
        packed = cols_all[1, m, p]
        return [
            jnp.concatenate(
                [
                    packed[:, (2 * place_of + b) * half : (2 * place_of + b + 1) * half]
                    for place_of in range(4)
                ],
                axis=1,
            )
            for b in range(2)
        ]

    def out_product(m, p):
        @pl.when(p == 0)
        def _():
            v_pairs(m).wait_recv()

        grad_cols(m, p).wait_recv()
        both = jnp.concatenate(grad_lanes(m, p), axis=0)
        for j in range(inner // (2 * TILE)):
            cols = slice(j * 2 * TILE, (j + 1) * 2 * TILE)
            acc[1, :, :, cols] += jnp.dot(
                both, rows_v[m, p, :, cols], preferred_element_type=jnp.float32
            ).reshape(2, share, 2 * TILE)

    def transpose_weights():
        def tile(j, carry):
            wvt_ref[:, tile_at(j)] = wv_ref[tile_at(j)].T
            return carry

        lax.fori_loop(0, wide, tile, 0)

    def stage(t, carry):
        at_top = top.astype(jnp.int32)
        lap, turn_of = t // (CHUNKS + 1), t % (CHUNKS + 1)
        chained = at_top * (turn_of < CHUNKS).astype(jnp.int32) + (1 - at_top) * (
            t >= micro
        ).astype(jnp.int32)
        k = at_top * (lap * CHUNKS + turn_of) + (1 - at_top) * (t - micro)
        m = at_top * lap + (1 - at_top) * t

        @pl.when(chained == 1)
        def _():
            @pl.when(jnp.logical_and(section < sections - 1, k == 0))
            def _():
                load_wo.wait()
                transpose_weights()

            @pl.when(jnp.logical_and(section == 0, k == 0))
            def _():
                acc[...] = jnp.zeros_like(acc)
                relay_values()

            chain(k)

            @pl.when(jnp.logical_and(section == 0, k > 0))
            def _():
                relay_grads(k - 1)

            @pl.when(
                jnp.logical_and(
                    section == 0, jnp.logical_and(k > CHUNKS, k % CHUNKS == 1)
                )
            )
            def _():
                value_product(k // CHUNKS - 1)

            @pl.when(
                jnp.logical_and(
                    section == 0,
                    jnp.logical_and(k > CHUNKS // 2, k % (CHUNKS // 2) == CHUNKS // 2 - 1),
                )
            )
            def _():
                unit = k // (CHUNKS // 2) - 1
                out_product(unit // 2, unit % 2)

        @pl.when(chained == 0)
        def _():
            values(m)

        return carry

    lax.fori_loop(0, steps + micro, stage, 0)
    gain_all[me] = jnp.sum(gain_part[...], axis=0, keepdims=True)
    for bits in range(1, peers):
        gain_copy(bits).start()

    @pl.when(section > 0)
    def _():
        acc[...] = jnp.zeros_like(acc)
        relay_values()

        def early(k, carry):
            relay_grads(k)
            return carry

        lax.fori_loop(0, steps - 1, early, 0)

        def heavy(m, carry):
            value_product(m)
            return carry

        lax.fori_loop(0, micro - 1, heavy, 0)

        def light(unit, carry):
            out_product(unit // 2, unit % 2)
            return carry

        lax.fori_loop(0, 2 * micro - 1, light, 0)

    relay_grads(steps - 1)
    last = micro - 1
    mine = coordinate(me, far[1])
    grad_cols(last, 1).wait_recv()
    lanes = grad_lanes(last, 1)
    give = jnp.where(mine == 0, lanes[1], lanes[0])
    keep = jnp.where(mine == 0, lanes[0], lanes[1])
    for j in range(narrow):
        cols = slice(j * TILE, (j + 1) * TILE)
        part_out[1, j] = (
            acc[1, 1 - mine, :, cols]
            + jnp.dot(give, rows_v[last, 1, :, cols], preferred_element_type=jnp.float32)
        ).astype(jnp.bfloat16)
        part_copy(1, j).start()

    side = coordinate(me, far[0])
    value_cols(last).wait_recv()
    gv_pairs(last).wait_recv()
    for j in range(narrow):
        cols = slice(j * TILE, (j + 1) * TILE)
        part_out[0, j] = (
            acc[0, 1 - side, :, cols]
            + jnp.dot(
                cols_all[0, last, 1 - side],
                rows_gv[last, :, cols],
                preferred_element_type=jnp.float32,
            )
        ).astype(jnp.bfloat16)
        part_copy(0, j).start()

    for j in range(narrow):
        cols = slice(j * TILE, (j + 1) * TILE)
        acc[1, mine, :, cols] += jnp.dot(
            keep, rows_v[last, 1, :, cols], preferred_element_type=jnp.float32
        )
        acc[0, side, :, cols] += jnp.dot(
            cols_all[0, last, side], rows_gv[last, :, cols], preferred_element_type=jnp.float32
        )

    gains().wait_recv()
    gained = gain_all[0]
    for owner in range(1, peers):
        gained = gained + gain_all[owner]
    gg_ref[...] = gained
    gv_all().wait_send()
    v_all().wait_send()
    for kind in (0, 1):
        cols_sent(kind).wait_send()

    @pl.when(section > 0)
    def _():
        remote(
            pass_buf, grad_buf, down_send.at[0], down_recv.at[0], {"section": section - 1}
        ).wait_send()

    gains().wait_send()
    for j in range(narrow):
        cols = slice(j * TILE, (j + 1) * TILE)
        for kind, row, out_ref in ((1, mine, og_ref), (0, side, vg_ref)):
            part_copy(kind, j).wait_recv()
            out_ref[:, cols] = acc[kind, row, :, cols] + part_in[kind, j].astype(jnp.float32)

    for kind in (0, 1):
        remote(
            part_out.at[kind], part_in.at[kind], part_send.at[kind], part_recv.at[kind, 0], peer(1)
        ).wait_send()


def fused(mesh, saved, cotangent, slot_table, gain, value_weight, out_weight):
    peers, sections = mesh.shape["seq"], mesh.shape["section"]
    micro, tokens, width = cotangent.shape
    inner = value_weight.shape[2]
    share = width // peers
    narrow = inner // TILE
    chunk = tokens // CHUNKS
    steps = micro * CHUNKS
    held = pl.BlockSpec(memory_space=pltpu.VMEM)
    far_off = pl.BlockSpec(memory_space=pl.ANY)
    value_grad, out_grad, gain_grad = pl.pallas_call(
        functools.partial(fused_kernel, peers, sections),
        out_shape=(
            jax.ShapeDtypeStruct((share, inner), jnp.float32),
            jax.ShapeDtypeStruct((share, inner), jnp.float32),
            jax.ShapeDtypeStruct((1, width), jnp.float32),
        ),
        in_specs=[
            pl.BlockSpec(memory_space=pltpu.SMEM),
            far_off,
            far_off,
            held,
            far_off,
            far_off,
        ],
        out_specs=(held, held, held),
        scratch_shapes=[
            pltpu.VMEM((micro, tokens, width), jnp.bfloat16),
            pltpu.VMEM((width, inner), jnp.bfloat16),
            pltpu.VMEM((width, inner), jnp.bfloat16),
            pltpu.VMEM((inner, width), jnp.bfloat16),
            pltpu.VMEM((micro, tokens, 1), jnp.float32),
            pltpu.VMEM((micro, tokens, width), jnp.bfloat16),
            pltpu.VMEM((micro, tokens, width), jnp.bfloat16),
            pltpu.VMEM((tokens, width), jnp.bfloat16),
            pltpu.VMEM((chunk, width), jnp.float32),
            pltpu.VMEM((micro, 4 * tokens, inner), jnp.bfloat16),
            pltpu.VMEM((micro, 2, 2 * tokens, inner), jnp.bfloat16),
            pltpu.VMEM((2, micro, width, tokens), jnp.bfloat16),
            pltpu.VMEM((2, micro, 2, share, 4 * tokens), jnp.bfloat16),
            pltpu.VMEM((2, 2, share, inner), jnp.float32),
            pltpu.VMEM((2, narrow, share, TILE), jnp.bfloat16),
            pltpu.VMEM((2, narrow, share, TILE), jnp.bfloat16),
            pltpu.VMEM((8, width), jnp.float32),
            pltpu.VMEM((peers, 1, width), jnp.float32),
            pltpu.SemaphoreType.DMA((4,)),
            pltpu.SemaphoreType.DMA((3,)),
            pltpu.SemaphoreType.DMA((1,)),
            pltpu.SemaphoreType.DMA((steps,)),
            pltpu.SemaphoreType.DMA((micro,)),
            pltpu.SemaphoreType.DMA((1,)),
            pltpu.SemaphoreType.DMA((micro,)),
            pltpu.SemaphoreType.DMA((micro,)),
            pltpu.SemaphoreType.DMA((2,)),
            pltpu.SemaphoreType.DMA((2, micro, 2)),
            pltpu.SemaphoreType.DMA((1,)),
            pltpu.SemaphoreType.DMA((steps,)),
            pltpu.SemaphoreType.DMA((2,)),
            pltpu.SemaphoreType.DMA((2, narrow)),
            pltpu.SemaphoreType.DMA((1,)),
            pltpu.SemaphoreType.DMA((1,)),
        ],
        compiler_params=pltpu.CompilerParams(
            collective_id=0, has_side_effects=True, vmem_limit_bytes=VMEM_BYTES
        ),
    )(slot_table, saved[0], cotangent, gain, value_weight[0], out_weight[0])
    return value_grad[None], out_grad[None], gain_grad


def fits(mesh, saved, cotangent, slot_table, gain, value_weight, out_weight):
    peers = mesh.shape["seq"]
    micro, tokens, width = cotangent.shape
    inner = value_weight.shape[2]
    share = width // peers
    held = 6 * width * inner + 2 * 2 * micro * 4 * tokens * (inner + 2 * share)
    held += 2 * micro * tokens * width * 5 + 6 * tokens * width
    held += share * inner * (4 * 4 + 4 * 2 + 4 * 2)
    return (
        peers == 8
        and micro > 1
        and tokens == LANES
        and width % (3 * TILE) == 0
        and inner % (2 * TILE) == 0
        and width % (16 * peers) == 0
        and held < VMEM_BYTES - 2 * 1024 * 1024
    )


def on_device(mesh, *arrays):
    if fits(mesh, *arrays):
        return fused(mesh, *arrays)
    return per_device(*arrays)


def solution(mesh):
    in_specs = (
        P("section", None, "seq", None),
        P(None, "seq", None),
        P("section", None),
        P("section", None),
        P("section", None, None),
        P("section", None, None),
    )
    out_specs = (P("section", "seq", None), P("section", "seq", None), P("section", None))
    return jax.shard_map(
        functools.partial(on_device, mesh), mesh=mesh, in_specs=in_specs, out_specs=out_specs, check_vma=False
    )
```

time: 99.5 us -> 91.2 us (0.917)
  Pallas kernels: 94.6 us -> 86.3 us
    pallas_call x1, Pallas kernels: 94.6 us -> 86.3 us  [fused(): pl.pallas_call(functools.partial(fused_kernel, peers, sections), out_shap...]
where the time goes in v3:
time: 91.2 us; the launch traced here: 90.9 us
  Pallas kernels  86.3 us (95%)
  local copies, waits for them, and re-layouts  3.97 us (4%)
    pallas_call x1, Pallas kernels, fused(): pl.pallas_call(functools.partial(fused_kernel, peers, sections), out_shap...  86.3 us
    unnamed x7, local copies, waits for them, and re-layouts  3.97 us

profile of v3, /device:TPU:0, one launch (start us, length us, event | category | flops | bytes accessed | tf_op | source)
XLA Modules:
  0.0 90.9 jit_solution(10280272710748943031)
XLA Ops:
  0.6 0.0 copy-start
  0.6 0.7 copy-done
  1.3 0.0 copy-start.1
  1.3 0.7 copy-done.1
  2.0 86.3 %shard_map.85 = (f32[288,1024]{1,0:T(8,128)S(1)}, f32[288,1024]{1,0:T(8,128)S(1)}, f32[1,2304]{1,0:T(1,128)S(1)}) custom-call(s32[1,3]{1,0:T(1,128)S(1)} %copy-done.1, bf16[3,128,2304]{2,1,0:T(8,128)(2,1)} %bitcast.9, bf16[3,128,2304]{2,1,0:T(8,128)(2,1)} %cot_hbm.1, f32[1,2304]{1,0:T(1,128)S(1)} %copy-done, bf16[2304,1024]{1,0:T(8,128)(2,1)} %bitcast.7, ...), custom_call_target="tpu_custom_call" | custom-call | tf_op jit(solution)/shard_map/pallas_call | solution.py:746
  88.3 1.0 %copy.12 = f32[1,288,1024]{2,1,0:T(8,128)} copy(f32[1,288,1024]{2,1,0:T(8,128)S(1)} %bitcast.6) | data formatting | bytes 2359296
  89.3 1.0 %copy.13 = f32[1,288,1024]{2,1,0:T(8,128)} copy(f32[1,288,1024]{2,1,0:T(8,128)S(1)} %bitcast.5) | data formatting | bytes 2359296
  90.3 0.6 copy.14
Async XLA Ops:
  0.6 0.7 copy-start
  1.3 0.7 copy-start.1

commit v4 on v3

--- a/solution.py
+++ b/solution.py
@@ -305,13 +305,13 @@
         spot = cols_all.at[kind, :, :, :, : 3 * tokens]
         return remote(spot, spot, cols_send.at[kind], cols_recv.at[kind, 0, 0], peer(1))
 
-    def down_copy(k, target):
-        spot = tile_at(k % CHUNKS, chunk)
+    def down_copy(k, g, target):
+        spot, cols = tile_at(k % CHUNKS, chunk), slice(g * third, (g + 1) * third)
         return remote(
-            pass_buf.at[k // CHUNKS, spot],
-            grad_buf.at[k // CHUNKS, spot],
+            pass_buf.at[k // CHUNKS, spot, cols],
+            grad_buf.at[k // CHUNKS, spot, cols],
             down_send.at[0],
-            down_recv.at[k],
+            down_recv.at[k, g],
             {"section": target},
         )
 
@@ -347,9 +347,6 @@
     def _():
         load_first.start()
         load_wo.start()
-        for j in range(3):
-            load_wv(j).start()
-        load_rest.start()
 
     @pl.when(section < sections - 1)
     def _():
@@ -396,6 +393,11 @@
 
     lax.fori_loop(0, micro, scales, 0)
 
+    @pl.when(top)
+    def _():
+        load_wv(0).start()
+        load_wv(1).start()
+
     pl.semaphore_wait(
         barrier,
         peers - 1
@@ -407,6 +409,8 @@
     def _():
         load_first.wait()
         load_wo.wait()
+        load_wv(2).start()
+        load_rest.start()
 
     @pl.when(section < sections - 1)
     def _():
@@ -448,6 +452,59 @@
         def _():
             send_cols(1, m, (1,))
 
+    def dispatch(k, count, grad_value):
+        m, h = k // CHUNKS, k % CHUNKS
+        spot = place(0, me) * CHUNKS + h
+        for i in range(count):
+            rows_gv[m, tile_at(spot + i, chunk)] = grad_value[i * chunk : (i + 1) * chunk].astype(
+                jnp.bfloat16
+            )
+        for i in range(count):
+            gv_to_chip(k + i).start()
+            gv_to_core(k + i).start()
+
+    def whole(k, count, first):
+        m, h = k // CHUNKS, k % CHUNKS
+        rows = count * chunk
+        here = tile_at(h // count, rows)
+        slot = slot_ref[0, m]
+        inv = inv_buf[m, here]
+        dispatch(
+            k,
+            count,
+            jnp.dot(grad_buf[m, here], wo_ref[...], preferred_element_type=jnp.float32),
+        )
+        grad_value = rows_gv[m, tile_at((place(0, me) * CHUNKS + h) // count, rows)]
+        total = jnp.zeros((rows, LANES), jnp.float32)
+        for j in range(3):
+            cols = slice(j * third, (j + 1) * third)
+            if first:
+                load_wv(j).wait()
+            term = lax.dot_general(
+                grad_value,
+                wv_ref[cols],
+                (((1,), (1,)), ((), ())),
+                preferred_element_type=jnp.float32,
+            )
+            unit = saved_ref[slot, here, cols].astype(jnp.float32) * inv
+            grad_unit = term * gain_ref[:, cols]
+            gn[:rows, cols] = grad_unit
+            gain_part[:, cols] += jnp.sum((term * unit).reshape(rows // 8, 8, third), axis=0)
+            both = grad_unit * unit
+            for i in range(third // LANES):
+                total = total + both[:, i * LANES : (i + 1) * LANES]
+        pull = inv * inv * (jnp.sum(total, axis=1, keepdims=True) / width)
+        for j in range(3):
+            cols = slice(j * third, (j + 1) * third)
+            pass_buf[m, here, cols] = (
+                grad_buf[m, here, cols].astype(jnp.float32)
+                + inv * gn[:rows, cols]
+                - saved_ref[slot, here, cols].astype(jnp.float32) * pull
+            ).astype(jnp.bfloat16)
+        for i in range(count):
+            for j in range(3):
+                down_copy(k + i, j, section - 1).start()
+
     def chain(k):
         m, h = k // CHUNKS, k % CHUNKS
         here = tile_at(h, chunk)
@@ -455,81 +512,57 @@
         inv = inv_buf[m, here]
         mine = tile_at(place(0, me) * CHUNKS + h, chunk)
         turning = (h % (CHUNKS // 2)) == CHUNKS // 2 - 1
-
-        @pl.when(section < sections - 1)
+        total = jnp.zeros((chunk, inner), jnp.float32)
+        for g in range(3):
+            cols = slice(g * third, (g + 1) * third)
+            down_copy(k, g, section + 1).wait_recv()
+            if g == 2:
+
+                @pl.when(jnp.logical_and(section == 0, turning))
+                def _():
+                    turn(m, h // (CHUNKS // 2))
+
+            total = total + jnp.dot(
+                grad_buf[m, here, cols], wo_ref[cols], preferred_element_type=jnp.float32
+            )
+        dispatch(k, 1, total)
+
+        @pl.when(section > 0)
         def _():
-            down_copy(k, section + 1).wait_recv()
-
-        @pl.when(jnp.logical_and(section == 0, turning))
-        def _():
-            turn(m, h // (CHUNKS // 2))
-
-        rows_gv[m, mine] = jnp.dot(
-            grad_buf[m, here], wo_ref[...], preferred_element_type=jnp.float32
-        ).astype(jnp.bfloat16)
-        gv_to_chip(k).start()
-        gv_to_core(k).start()
-
-        def back(flip, first):
             grad_value = rows_gv[m, mine]
-            total = jnp.zeros((chunk, LANES), jnp.float32)
+            own = place(1, me) * (CHUNKS // 2) + h % (CHUNKS // 2)
+            value = rows_v[m, h // (CHUNKS // 2), tile_at(own, chunk)]
+            dots = jnp.sum(
+                grad_value.astype(jnp.float32) * value.astype(jnp.float32), axis=1, keepdims=True
+            )
+            pull = inv * inv * (dots / width)
             for j in range(3):
                 cols = slice(j * third, (j + 1) * third)
-                if flip:
-                    if first:
-                        load_wv(j).wait()
-                    term = lax.dot_general(
-                        grad_value,
-                        wv_ref[cols],
-                        (((1,), (1,)), ((), ())),
-                        preferred_element_type=jnp.float32,
-                    )
-                else:
-                    term = jnp.dot(
-                        grad_value, wvt_ref[:, cols], preferred_element_type=jnp.float32
-                    )
-                unit = saved_ref[slot, here, cols].astype(jnp.float32) * inv
-                grad_unit = term * gain_ref[:, cols]
-                gn[:, cols] = grad_unit
-                gain_part[:, cols] += jnp.sum(
-                    (term * unit).reshape(chunk // 8, 8, third), axis=0
-                )
-                both = grad_unit * unit
-                for i in range(third // LANES):
-                    total = total + both[:, i * LANES : (i + 1) * LANES]
-            return jnp.sum(total, axis=1, keepdims=True) / width
-
-        def down(mean):
-            pull = inv * inv * mean
-            for j in range(wide):
-                cols = slice(j * TILE, (j + 1) * TILE)
+                term = jnp.dot(grad_value, wvt_ref[:, cols], preferred_element_type=jnp.float32)
+                x = saved_ref[slot, here, cols].astype(jnp.float32)
                 pass_buf[m, here, cols] = (
                     grad_buf[m, here, cols].astype(jnp.float32)
-                    + inv * gn[:, cols]
-                    - saved_ref[slot, here, cols].astype(jnp.float32) * pull
+                    + inv * (term * gain_ref[:, cols])
+                    - x * pull
                 ).astype(jnp.bfloat16)
-            down_copy(k, section - 1).start()
-
-        @pl.when(jnp.logical_and(top, k == 0))
-        def _():
-            down(back(True, True))
-            load_rest.wait()
-
-        @pl.when(jnp.logical_and(top, k > 0))
-        def _():
-            down(back(True, False))
-
-        @pl.when(section < sections - 1)
-        def _():
-            mean = back(False, False)
-
-            @pl.when(section > 0)
-            def _():
-                down(mean)
+                down_copy(k, j, section - 1).start()
+                gain_part[:, cols] += jnp.sum(
+                    (term * (x * inv)).reshape(chunk // 8, 8, third), axis=0
+                )
 
         @pl.when(jnp.logical_and(section > 0, turning))
         def _():
             turn(m, h // (CHUNKS // 2))
+
+    def gain_terms(m):
+        slot = slot_ref[0, m]
+        inv = inv_buf[m]
+        grad_value = rows_gv[m, tile_at(place(0, me), tokens)]
+        for j in range(3):
+            cols = slice(j * third, (j + 1) * third)
+            term = jnp.dot(grad_value, wvt_ref[:, cols], preferred_element_type=jnp.float32)
+            unit = saved_ref[slot, :, cols].astype(jnp.float32) * inv
+            gain_part[:, cols] += jnp.sum((term * unit).reshape(tokens // 8, 8, third), axis=0)
 
     def relay_values():
         def one(m, carry):
@@ -586,18 +619,31 @@
 
         lax.fori_loop(0, wide, tile, 0)
 
+    @pl.when(top)
+    def _():
+        whole(0, 1, True)
+        load_rest.wait()
+        whole(1, 1, False)
+        turn(0, 0)
+
+        def pair(unit, carry):
+            whole(unit * (CHUNKS // 2), CHUNKS // 2, False)
+            turn(unit // 2, unit % 2)
+
+            @pl.when(unit <= micro)
+            def _():
+                values(unit - 1)
+
+            return carry
+
+        lax.fori_loop(1, 2 * micro, pair, 0)
+
     def stage(t, carry):
-        at_top = top.astype(jnp.int32)
-        lap, turn_of = t // (CHUNKS + 1), t % (CHUNKS + 1)
-        chained = at_top * (turn_of < CHUNKS).astype(jnp.int32) + (1 - at_top) * (
-            t >= micro
-        ).astype(jnp.int32)
-        k = at_top * (lap * CHUNKS + turn_of) + (1 - at_top) * (t - micro)
-        m = at_top * lap + (1 - at_top) * t
-
-        @pl.when(chained == 1)
+        k = t - micro
+
+        @pl.when(k >= 0)
         def _():
-            @pl.when(jnp.logical_and(section < sections - 1, k == 0))
+            @pl.when(k == 0)
             def _():
                 load_wo.wait()
                 transpose_weights()
@@ -609,17 +655,25 @@
 
             chain(k)
 
-            @pl.when(jnp.logical_and(section == 0, k > 0))
+            @pl.when(jnp.logical_and(section == 0, k > 1))
             def _():
-                relay_grads(k - 1)
+                relay_grads(k - 2)
 
             @pl.when(
                 jnp.logical_and(
-                    section == 0, jnp.logical_and(k > CHUNKS, k % CHUNKS == 1)
+                    section == 0, jnp.logical_and(k > CHUNKS, k % CHUNKS == 2)
                 )
             )
             def _():
                 value_product(k // CHUNKS - 1)
+
+            @pl.when(
+                jnp.logical_and(
+                    section == 0, jnp.logical_and(k >= CHUNKS, k % CHUNKS == 0)
+                )
+            )
+            def _():
+                gain_terms(k // CHUNKS - 1)
 
             @pl.when(
                 jnp.logical_and(
@@ -631,13 +685,21 @@
                 unit = k // (CHUNKS // 2) - 1
                 out_product(unit // 2, unit % 2)
 
-        @pl.when(chained == 0)
+        @pl.when(k < 0)
         def _():
-            values(m)
+            values(t)
 
         return carry
 
-    lax.fori_loop(0, steps + micro, stage, 0)
+    @pl.when(section < sections - 1)
+    def _():
+        lax.fori_loop(0, steps + micro, stage, 0)
+
+    @pl.when(section == 0)
+    def _():
+        relay_grads(steps - 2)
+        gain_terms(micro - 1)
+
     gain_all[me] = jnp.sum(gain_part[...], axis=0, keepdims=True)
     for bits in range(1, peers):
         gain_copy(bits).start()
@@ -672,6 +734,9 @@
     lanes = grad_lanes(last, 1)
     give = jnp.where(mine == 0, lanes[1], lanes[0])
     keep = jnp.where(mine == 0, lanes[0], lanes[1])
+    side = coordinate(me, far[0])
+    value_cols(last).wait_recv()
+    gv_pairs(last).wait_recv()
     for j in range(narrow):
         cols = slice(j * TILE, (j + 1) * TILE)
         part_out[1, j] = (
@@ -679,12 +744,6 @@
             + jnp.dot(give, rows_v[last, 1, :, cols], preferred_element_type=jnp.float32)
         ).astype(jnp.bfloat16)
         part_copy(1, j).start()
-
-    side = coordinate(me, far[0])
-    value_cols(last).wait_recv()
-    gv_pairs(last).wait_recv()
-    for j in range(narrow):
-        cols = slice(j * TILE, (j + 1) * TILE)
         part_out[0, j] = (
             acc[0, 1 - side, :, cols]
             + jnp.dot(
@@ -717,7 +776,7 @@
     @pl.when(section > 0)
     def _():
         remote(
-            pass_buf, grad_buf, down_send.at[0], down_recv.at[0], {"section": section - 1}
+            pass_buf, grad_buf, down_send.at[0], down_recv.at[0, 0], {"section": section - 1}
         ).wait_send()
 
     gains().wait_send()
@@ -731,6 +790,18 @@
         remote(
             part_out.at[kind], part_in.at[kind], part_send.at[kind], part_recv.at[kind, 0], peer(1)
         ).wait_send()
+
+
+def place_outputs(vg_ref, og_ref, gg_ref, vg_out, og_out, gg_out, sem):
+    pairs = ((vg_ref, vg_out), (og_ref, og_out), (gg_ref, gg_out))
+    copies = [
+        pltpu.make_async_copy(source, target, sem.at[i])
+        for i, (source, target) in enumerate(pairs)
+    ]
+    for copy in copies:
+        copy.start()
+    for copy in copies:
+        copy.wait()
 
 
 def fused(mesh, saved, cotangent, slot_table, gain, value_weight, out_weight):
@@ -768,7 +839,7 @@
             pltpu.VMEM((micro, tokens, width), jnp.bfloat16),
             pltpu.VMEM((micro, tokens, width), jnp.bfloat16),
             pltpu.VMEM((tokens, width), jnp.bfloat16),
-            pltpu.VMEM((chunk, width), jnp.float32),
+            pltpu.VMEM((tokens // 2, width), jnp.float32),
             pltpu.VMEM((micro, 4 * tokens, inner), jnp.bfloat16),
             pltpu.VMEM((micro, 2, 2 * tokens, inner), jnp.bfloat16),
             pltpu.VMEM((2, micro, width, tokens), jnp.bfloat16),
@@ -789,7 +860,7 @@
             pltpu.SemaphoreType.DMA((2,)),
             pltpu.SemaphoreType.DMA((2, micro, 2)),
             pltpu.SemaphoreType.DMA((1,)),
-            pltpu.SemaphoreType.DMA((steps,)),
+            pltpu.SemaphoreType.DMA((steps, 3)),
             pltpu.SemaphoreType.DMA((2,)),
             pltpu.SemaphoreType.DMA((2, narrow)),
             pltpu.SemaphoreType.DMA((1,)),
@@ -799,6 +870,18 @@
             collective_id=0, has_side_effects=True, vmem_limit_bytes=VMEM_BYTES
         ),
     )(slot_table, saved[0], cotangent, gain, value_weight[0], out_weight[0])
+    value_grad, out_grad, gain_grad = pl.pallas_call(
+        place_outputs,
+        out_shape=(
+            jax.ShapeDtypeStruct((share, inner), jnp.float32),
+            jax.ShapeDtypeStruct((share, inner), jnp.float32),
+            jax.ShapeDtypeStruct((1, width), jnp.float32),
+        ),
+        in_specs=[far_off] * 3,
+        out_specs=(far_off,) * 3,
+        scratch_shapes=[pltpu.SemaphoreType.DMA((3,))],
+        compiler_params=pltpu.CompilerParams(vmem_limit_bytes=8 * 1024 * 1024),
+    )(value_grad, out_grad, gain_grad)
     return value_grad[None], out_grad[None], gain_grad
 
 

time: 91.2 us -> 85.1 us (0.933)
  Pallas kernels: 86.3 us -> 82.7 us
  local copies, waits for them, and re-layouts: 3.97 us -> 1.35 us
    pallas_call x1, Pallas kernels: 86.3 us -> 81.2 us  [fused(): pl.pallas_call(functools.partial(fused_kernel, peers, sections), out_shap...]
    unnamed x7 -> x4, local copies, waits for them, and re-layouts: 3.97 us -> 1.35 us
    pallas_call x0 -> x1, Pallas kernels: none -> 1.43 us  [fused(): pl.pallas_call(place_outputs, out_shape=(jax.ShapeDtypeStruct((share, inn...]
where the time goes in v4:
time: 85.1 us; the launch traced here: 84.8 us
  Pallas kernels  82.7 us (97%)
  local copies, waits for them, and re-layouts  1.35 us (2%)
    pallas_call x1, Pallas kernels, fused(): pl.pallas_call(functools.partial(fused_kernel, peers, sections), out_shap...  81.2 us

profile of v4, /device:TPU:0, one launch (start us, length us, event | category | flops | bytes accessed | tf_op | source)
XLA Modules:
  0.0 84.8 jit_solution(10468562443044412371)
XLA Ops:
  0.6 0.0 copy-start
  0.6 0.7 copy-done
  1.3 0.0 copy-start.1
  1.3 0.7 copy-done.1
  2.0 81.2 %shard_map.85 = (f32[288,1024]{1,0:T(8,128)S(1)}, f32[288,1024]{1,0:T(8,128)S(1)}, f32[1,2304]{1,0:T(1,128)S(1)}) custom-call(s32[1,3]{1,0:T(1,128)S(1)} %copy-done.1, bf16[3,128,2304]{2,1,0:T(8,128)(2,1)} %bitcast.7, bf16[3,128,2304]{2,1,0:T(8,128)(2,1)} %cot_hbm.1, f32[1,2304]{1,0:T(1,128)S(1)} %copy-done, bf16[2304,1024]{1,0:T(8,128)(2,1)} %bitcast.5, ...), custom_call_target="tpu_custom_call" | custom-call | tf_op jit(solution)/shard_map/pallas_call | solution.py:817
  83.2 1.4 %shard_map.86 = (f32[288,1024]{1,0:T(8,128)}, f32[288,1024]{1,0:T(8,128)}, f32[1,2304]{1,0:T(1,128)}) custom-call(f32[288,1024]{1,0:T(8,128)S(1)} %get-tuple-element.9.vg_ref, f32[288,1024]{1,0:T(8,128)S(1)} %get-tuple-element.10.og_ref, f32[1,2304]{1,0:T(1,128)S(1)} %get-tuple-element.11.gg_ref), custom_call_target="tpu_custom_call" | custom-call | tf_op jit(solution)/shard_map/pallas_call | solution.py:873
Async XLA Ops:
  0.6 0.7 copy-start
  1.3 0.7 copy-start.1

commit v5 on v4

--- a/solution.py
+++ b/solution.py
@@ -140,7 +140,7 @@
 def fused_kernel(
     peers,
     sections,
-    slot_ref,
+    slot_hbm,
     saved_hbm,
     cot_hbm,
     gain_ref,
@@ -167,6 +167,7 @@
     part_in,
     gain_part,
     gain_all,
+    slot_ref,
     load_sem,
     wv_sem,
     gv_send,
@@ -191,6 +192,8 @@
     share = width // peers
     wide, narrow = width // TILE, inner // TILE
     third = width // 3
+    edges = [TILE * at for at in (0, wide // 3, wide - wide // 3, wide)]
+    groups = [slice(low, high) for low, high in zip(edges[:-1], edges[1:])]
     chunk, half = tokens // CHUNKS, tokens // 2
     steps = micro * CHUNKS
     top = section == sections - 1
@@ -306,7 +309,7 @@
         return remote(spot, spot, cols_send.at[kind], cols_recv.at[kind, 0, 0], peer(1))
 
     def down_copy(k, g, target):
-        spot, cols = tile_at(k % CHUNKS, chunk), slice(g * third, (g + 1) * third)
+        spot, cols = tile_at(k % CHUNKS, chunk), groups[g]
         return remote(
             pass_buf.at[k // CHUNKS, spot, cols],
             grad_buf.at[k // CHUNKS, spot, cols],
@@ -333,6 +336,7 @@
         return remote(spot, spot, gain_send.at[0], gain_recv.at[0], peer(1))
 
     load_saved = pltpu.make_async_copy(saved_hbm, saved_ref, load_sem.at[0])
+    load_slot = pltpu.make_async_copy(slot_hbm, slot_ref, load_sem.at[4])
     load_wo = pltpu.make_async_copy(wo_hbm, wo_ref, load_sem.at[1])
     load_first = pltpu.make_async_copy(cot_hbm.at[0], grad_buf.at[0], load_sem.at[2])
     load_rest = pltpu.make_async_copy(cot_hbm.at[1:], grad_buf.at[1:], load_sem.at[3])
@@ -341,8 +345,6 @@
         rows = slice(j * third, (j + 1) * third)
         return pltpu.make_async_copy(wv_hbm.at[rows], wv_ref.at[rows], wv_sem.at[j])
 
-    load_saved.start()
-
     @pl.when(top)
     def _():
         load_first.start()
@@ -350,10 +352,12 @@
 
     @pl.when(section < sections - 1)
     def _():
+        load_saved.start()
         for j in range(3):
             load_wv(j).start()
         load_wo.start()
 
+    load_slot.start()
     barrier = pltpu.get_barrier_semaphore()
     for bits in range(1, peers):
         pl.semaphore_signal(
@@ -379,7 +383,18 @@
         )
 
     gain_part[...] = jnp.zeros_like(gain_part)
-    load_saved.wait()
+
+    @pl.when(top)
+    def _():
+        load_first.wait()
+        load_saved.start()
+        load_wv(0).start()
+
+    @pl.when(section < sections - 1)
+    def _():
+        load_saved.wait()
+
+    load_slot.wait()
 
     def scales(m, carry):
         slot = slot_ref[0, m]
@@ -391,12 +406,9 @@
         inv_buf[m] = lax.rsqrt(total / width + EPSILON)
         return carry
 
-    lax.fori_loop(0, micro, scales, 0)
-
-    @pl.when(top)
-    def _():
-        load_wv(0).start()
-        load_wv(1).start()
+    @pl.when(section < sections - 1)
+    def _():
+        lax.fori_loop(0, micro, scales, 0)
 
     pl.semaphore_wait(
         barrier,
@@ -407,8 +419,8 @@
 
     @pl.when(top)
     def _():
-        load_first.wait()
         load_wo.wait()
+        load_wv(1).start()
         load_wv(2).start()
         load_rest.start()
 
@@ -468,12 +480,15 @@
         rows = count * chunk
         here = tile_at(h // count, rows)
         slot = slot_ref[0, m]
-        inv = inv_buf[m, here]
         dispatch(
             k,
             count,
             jnp.dot(grad_buf[m, here], wo_ref[...], preferred_element_type=jnp.float32),
         )
+        if first:
+            load_saved.wait()
+            scales(0, 0)
+        inv = inv_buf[m, here]
         grad_value = rows_gv[m, tile_at((place(0, me) * CHUNKS + h) // count, rows)]
         total = jnp.zeros((rows, LANES), jnp.float32)
         for j in range(3):
@@ -502,8 +517,8 @@
                 - saved_ref[slot, here, cols].astype(jnp.float32) * pull
             ).astype(jnp.bfloat16)
         for i in range(count):
-            for j in range(3):
-                down_copy(k + i, j, section - 1).start()
+            for g in range(len(groups)):
+                down_copy(k + i, g, section - 1).start()
 
     def chain(k):
         m, h = k // CHUNKS, k % CHUNKS
@@ -513,10 +528,9 @@
         mine = tile_at(place(0, me) * CHUNKS + h, chunk)
         turning = (h % (CHUNKS // 2)) == CHUNKS // 2 - 1
         total = jnp.zeros((chunk, inner), jnp.float32)
-        for g in range(3):
-            cols = slice(g * third, (g + 1) * third)
+        for g, cols in enumerate(groups):
             down_copy(k, g, section + 1).wait_recv()
-            if g == 2:
+            if g == len(groups) - 1:
 
                 @pl.when(jnp.logical_and(section == 0, turning))
                 def _():
@@ -536,8 +550,7 @@
                 grad_value.astype(jnp.float32) * value.astype(jnp.float32), axis=1, keepdims=True
             )
             pull = inv * inv * (dots / width)
-            for j in range(3):
-                cols = slice(j * third, (j + 1) * third)
+            for g, cols in enumerate(groups):
                 term = jnp.dot(grad_value, wvt_ref[:, cols], preferred_element_type=jnp.float32)
                 x = saved_ref[slot, here, cols].astype(jnp.float32)
                 pass_buf[m, here, cols] = (
@@ -545,9 +558,9 @@
                     + inv * (term * gain_ref[:, cols])
                     - x * pull
                 ).astype(jnp.bfloat16)
-                down_copy(k, j, section - 1).start()
+                down_copy(k, g, section - 1).start()
                 gain_part[:, cols] += jnp.sum(
-                    (term * (x * inv)).reshape(chunk // 8, 8, third), axis=0
+                    (term * (x * inv)).reshape(chunk // 8, 8, cols.stop - cols.start), axis=0
                 )
 
         @pl.when(jnp.logical_and(section > 0, turning))
@@ -622,6 +635,7 @@
     @pl.when(top)
     def _():
         whole(0, 1, True)
+        lax.fori_loop(1, micro, scales, 0)
         load_rest.wait()
         whole(1, 1, False)
         turn(0, 0)
@@ -735,8 +749,6 @@
     give = jnp.where(mine == 0, lanes[1], lanes[0])
     keep = jnp.where(mine == 0, lanes[0], lanes[1])
     side = coordinate(me, far[0])
-    value_cols(last).wait_recv()
-    gv_pairs(last).wait_recv()
     for j in range(narrow):
         cols = slice(j * TILE, (j + 1) * TILE)
         part_out[1, j] = (
@@ -744,6 +756,9 @@
             + jnp.dot(give, rows_v[last, 1, :, cols], preferred_element_type=jnp.float32)
         ).astype(jnp.bfloat16)
         part_copy(1, j).start()
+        if j == 0:
+            value_cols(last).wait_recv()
+            gv_pairs(last).wait_recv()
         part_out[0, j] = (
             acc[0, 1 - side, :, cols]
             + jnp.dot(
@@ -822,7 +837,7 @@
             jax.ShapeDtypeStruct((1, width), jnp.float32),
         ),
         in_specs=[
-            pl.BlockSpec(memory_space=pltpu.SMEM),
+            far_off,
             far_off,
             far_off,
             held,
@@ -849,7 +864,8 @@
             pltpu.VMEM((2, narrow, share, TILE), jnp.bfloat16),
             pltpu.VMEM((8, width), jnp.float32),
             pltpu.VMEM((peers, 1, width), jnp.float32),
-            pltpu.SemaphoreType.DMA((4,)),
+            pltpu.SMEM((1, micro), jnp.int32),
+            pltpu.SemaphoreType.DMA((5,)),
             pltpu.SemaphoreType.DMA((3,)),
             pltpu.SemaphoreType.DMA((1,)),
             pltpu.SemaphoreType.DMA((steps,)),
@@ -898,6 +914,7 @@
         and micro > 1
         and tokens == LANES
         and width % (3 * TILE) == 0
+        and width >= 6 * TILE
         and inner % (2 * TILE) == 0
         and width % (16 * peers) == 0
         and held < VMEM_BYTES - 2 * 1024 * 1024

time: 85.1 us -> 84.9 us (level)
  no operation moved by 1% of the time
where the time goes in v5:
time: 84.9 us; the launch traced here: 84.6 us
  Pallas kernels  82.5 us (97%)
  local copies, waits for them, and re-layouts  1.35 us (2%)
    pallas_call x1, Pallas kernels, fused(): pl.pallas_call(functools.partial(fused_kernel, peers, sections), out_shap...  81 us

profile of v5, /device:TPU:0, one launch (start us, length us, event | category | flops | bytes accessed | tf_op | source)
XLA Modules:
  0.0 84.6 jit_solution(8447352012620118894)
XLA Ops:
  0.6 0.0 copy-start
  0.6 0.7 copy-done
  1.3 0.0 copy-start.1
  1.3 0.7 copy-done.1
  2.0 81.0 %shard_map.85 = (f32[288,1024]{1,0:T(8,128)S(1)}, f32[288,1024]{1,0:T(8,128)S(1)}, f32[1,2304]{1,0:T(1,128)S(1)}) custom-call(s32[1,3]{1,0:T(1,128)S(1)} %copy-done.1, bf16[3,128,2304]{2,1,0:T(8,128)(2,1)} %bitcast.7, bf16[3,128,2304]{2,1,0:T(8,128)(2,1)} %cot_hbm.1, f32[1,2304]{1,0:T(1,128)S(1)} %copy-done, bf16[2304,1024]{1,0:T(8,128)(2,1)} %bitcast.5, ...), custom_call_target="tpu_custom_call" | custom-call | tf_op jit(solution)/shard_map/pallas_call | solution.py:832
  83.0 1.4 %shard_map.86 = (f32[288,1024]{1,0:T(8,128)}, f32[288,1024]{1,0:T(8,128)}, f32[1,2304]{1,0:T(1,128)}) custom-call(f32[288,1024]{1,0:T(8,128)S(1)} %get-tuple-element.9.vg_ref, f32[288,1024]{1,0:T(8,128)S(1)} %get-tuple-element.10.og_ref, f32[1,2304]{1,0:T(1,128)S(1)} %get-tuple-element.11.gg_ref), custom_call_target="tpu_custom_call" | custom-call | tf_op jit(solution)/shard_map/pallas_call | solution.py:889
Async XLA Ops:
  0.6 0.7 copy-start
  1.3 0.7 copy-start.1

commit v6 on v5

--- a/solution.py
+++ b/solution.py
@@ -438,12 +438,14 @@
             n = (x * inv * gain_ref[:, cols]).astype(jnp.bfloat16)
             normed[:, cols] = n
             turned[0, m, cols] = n.T
-        send_cols(0, m, (0, 1))
         result = jnp.dot(
             normed[...], wv_ref[...], preferred_element_type=jnp.float32
         ).astype(jnp.bfloat16)
         for p in range(2):
             rows_v[m, p, tile_at(place(1, me), half)] = result[p * half : (p + 1) * half]
+
+    def share_values(m):
+        send_cols(0, m, (0, 1))
         v_to_chip(m).start()
         v_to_core(m).start()
 
@@ -647,6 +649,7 @@
             @pl.when(unit <= micro)
             def _():
                 values(unit - 1)
+                share_values(unit - 1)
 
             return carry
 
@@ -669,6 +672,14 @@
 
             chain(k)
 
+            @pl.when(
+                jnp.logical_and(
+                    section > 0, jnp.logical_and(k % CHUNKS == 1, k < CHUNKS * (micro - 1))
+                )
+            )
+            def _():
+                share_values(k // CHUNKS + 1)
+
             @pl.when(jnp.logical_and(section == 0, k > 1))
             def _():
                 relay_grads(k - 2)
@@ -702,6 +713,10 @@
         @pl.when(k < 0)
         def _():
             values(t)
+
+            @pl.when(jnp.logical_or(section == 0, t == 0))
+            def _():
+                share_values(t)
 
         return carry
 

time: 84.9 us -> 84.9 us (level)
  no operation moved by 1% of the time
where the time goes in v6:
time: 84.9 us; the launch traced here: 84.6 us
  Pallas kernels  82.5 us (97%)
  local copies, waits for them, and re-layouts  1.35 us (2%)
    pallas_call x1, Pallas kernels, fused(): pl.pallas_call(functools.partial(fused_kernel, peers, sections), out_shap...  81 us

profile of v6, /device:TPU:0, one launch (start us, length us, event | category | flops | bytes accessed | tf_op | source)
XLA Modules:
  0.0 84.6 jit_solution(11270880420266155160)
XLA Ops:
  0.6 0.0 copy-start
  0.6 0.7 copy-done
  1.3 0.0 copy-start.1
  1.3 0.7 copy-done.1
  2.0 81.0 %shard_map.85 = (f32[288,1024]{1,0:T(8,128)S(1)}, f32[288,1024]{1,0:T(8,128)S(1)}, f32[1,2304]{1,0:T(1,128)S(1)}) custom-call(s32[1,3]{1,0:T(1,128)S(1)} %copy-done.1, bf16[3,128,2304]{2,1,0:T(8,128)(2,1)} %bitcast.7, bf16[3,128,2304]{2,1,0:T(8,128)(2,1)} %cot_hbm.1, f32[1,2304]{1,0:T(1,128)S(1)} %copy-done, bf16[2304,1024]{1,0:T(8,128)(2,1)} %bitcast.5, ...), custom_call_target="tpu_custom_call" | custom-call | tf_op jit(solution)/shard_map/pallas_call | solution.py:847
  83.0 1.4 %shard_map.86 = (f32[288,1024]{1,0:T(8,128)}, f32[288,1024]{1,0:T(8,128)}, f32[1,2304]{1,0:T(1,128)}) custom-call(f32[288,1024]{1,0:T(8,128)S(1)} %get-tuple-element.9.vg_ref, f32[288,1024]{1,0:T(8,128)S(1)} %get-tuple-element.10.og_ref, f32[1,2304]{1,0:T(1,128)S(1)} %get-tuple-element.11.gg_ref), custom_call_target="tpu_custom_call" | custom-call | tf_op jit(solution)/shard_map/pallas_call | solution.py:904
Async XLA Ops:
  0.6 0.7 copy-start
  1.3 0.7 copy-start.1
